TPU v7x, 8 devices: a whole 2x2x1 slice. The times are simulated.
8 devices in a mesh: nodes: 8 (over z, y, x, core).
Axes of the slice: x: 2, y: 2, z: 1, core: 2. Of those that a mesh axis runs over, the one named last changes fastest.
Arguments:
- adjacency: bfloat16 [16384, 16384], P('nodes')
- features: bfloat16 [16384, 602], P('nodes')
- w_hidden: float32 [602, 128], replicated
- w_output: float32 [128, 41], replicated
- labels: int32 [16384], P('nodes')
- train_mask: int32 [16384], P('nodes')
- block_mask: int32 [8, 8], replicated
Outputs:
- output 1: float32 [], replicated
- output 2: float32 [602, 128], replicated
- output 3: float32 [128, 41], replicated
All inputs are finite; a program needn't handle non-finite values.
Results may differ from a plain program's by a relative error of at most 0.001.
Values are sent between devices in bfloat16 or wider.
A program may use at most 1 GiB of HBM per device.

v0:
```python
import jax
import jax.numpy as jnp
from jax import lax
from jax.sharding import PartitionSpec as P

AXIS_NAME = 'nodes'
ROW_CONTRACT = (((0,), (0,)), ((), ()))
LAST_CONTRACT = (((1,), (1,)), ((), ()))


def gather_masked(local_vals, mask_row):
    gathered = lax.all_gather(local_vals, AXIS_NAME, axis=0, tiled=False)
    gathered = gathered * mask_row.astype(local_vals.dtype)[:, None, None]
    return gathered.reshape(-1, local_vals.shape[-1])


def transpose_product_scatter(adj_rows, local_grad, mask_row):
    width = local_grad.shape[-1]
    contrib = lax.dot_general(adj_rows, local_grad, ROW_CONTRACT, preferred_element_type=jnp.float32)
    contrib = contrib.reshape(mask_row.shape[0], -1, width) * mask_row.astype(jnp.float32)[:, None, None]
    return lax.psum_scatter(contrib.reshape(-1, width), AXIS_NAME, scatter_dimension=0, tiled=True)


def device_step(adj_rows, feat_rows, w_hidden, w_output, labels, train_mask, block_mask):
    dev_index = lax.axis_index(AXIS_NAME)
    mask_row = lax.dynamic_index_in_dim(block_mask, dev_index, axis=0, keepdims=False)
    w_hidden_bf = w_hidden.astype(jnp.bfloat16)
    w_output_bf = w_output.astype(jnp.bfloat16)
    proj_one = jnp.dot(feat_rows, w_hidden_bf, preferred_element_type=jnp.float32).astype(jnp.bfloat16)
    agg_one = jnp.dot(adj_rows, gather_masked(proj_one, mask_row), preferred_element_type=jnp.float32)
    hidden = jnp.maximum(agg_one, 0.0).astype(jnp.bfloat16)
    proj_two = jnp.dot(hidden, w_output_bf, preferred_element_type=jnp.float32).astype(jnp.bfloat16)
    logits = jnp.dot(adj_rows, gather_masked(proj_two, mask_row), preferred_element_type=jnp.float32)
    label_weight = train_mask.astype(jnp.float32)
    log_norm = jax.nn.logsumexp(logits, axis=-1)
    one_hot = (labels[:, None] == jnp.arange(logits.shape[-1])[None, :]).astype(jnp.float32)
    picked = jnp.sum(logits * one_hot, axis=-1)
    totals = lax.psum(jnp.stack([jnp.sum(label_weight), jnp.sum(label_weight * (log_norm - picked))]), AXIS_NAME)
    label_count = totals[0]
    mean_loss = totals[1] / label_count
    probabilities = jnp.exp(logits - log_norm[:, None])
    grad_logits = ((probabilities - one_hot) * (label_weight / label_count)[:, None]).astype(jnp.bfloat16)
    grad_proj_two = transpose_product_scatter(adj_rows, grad_logits, mask_row).astype(jnp.bfloat16)
    grad_w_output = lax.psum(lax.dot_general(hidden, grad_proj_two, ROW_CONTRACT, preferred_element_type=jnp.float32), AXIS_NAME)
    grad_hidden = lax.dot_general(grad_proj_two, w_output_bf, LAST_CONTRACT, preferred_element_type=jnp.float32)
    grad_agg = jnp.where(agg_one > 0, grad_hidden, 0.0).astype(jnp.bfloat16)
    grad_proj_one = transpose_product_scatter(adj_rows, grad_agg, mask_row).astype(jnp.bfloat16)
    grad_w_hidden = lax.psum(lax.dot_general(feat_rows, grad_proj_one, ROW_CONTRACT, preferred_element_type=jnp.float32), AXIS_NAME)
    return mean_loss, grad_w_hidden, grad_w_output


def solution(mesh):
    row_spec = P(AXIS_NAME, None)
    vec_spec = P(AXIS_NAME)
    return jax.shard_map(device_step, mesh=mesh, in_specs=(row_spec, row_spec, P(), P(), vec_spec, vec_spec, P()), out_specs=(P(), P(), P()), check_vma=False)
```

profile of v0, /device:TPU:0, one launch (start us, length us, event | category | flops | bytes accessed | tf_op | source)
XLA Modules:
  0.0 373.9 jit_solution(12395351367350379846)
XLA Ops:
  7.2 1.6 copy-done
  8.9 2.7 convolution_convert_fusion
  11.6 0.0 all-gather.7.cloned.1.call-start
  11.6 0.7 convert_bitcast_fusion
  12.3 33.0 %all-gather.5.cloned.1.call-done = bf16[16384,128]{1,0:T(8,128)(2,1)} async-done(((bf16[2048,128]{1,0:T(8,128)(2,1)}), bf16[16384,128]{1,0:T(8,128)(2,1)}) %all-gather.5.cloned.1.call-update) | async-done | bytes 4194320 | tf_op jit(solution)/shard_map/all_gather | solution.py:12
  45.3 4.5 %broadcast_multiply_fusion = bf16[8,2048,128]{2,1,0:T(8,128)(2,1)} fusion(bf16[8,2048,128]{2,1,0:T(8,128)(2,1)} %bitcast.69, bf16[8]{0:T(256)(128)(2,1)S(1)} %get-tuple-element.9), kind=kLoop, calls=%fused_computation.8 | loop fusion | flops 2097152 | bytes 8388624 | tf_op jit(solution)/shard_map/mul | solution.py:13
  49.8 29.5 %fusion.33 = f32[128,2048]{1,0:T(8,128)S(1)} fusion(bf16[16384,128]{1,0:T(8,128)(2,1)} %bitcast.65, bf16[2048,16384]{1,0:T(8,128)(2,1)} %param.7), kind=kOutput, calls=%fused_computation.53 | convolution fusion | flops 8589934592 | bytes 72351744 | tf_op jit(solution)/shard_map/dot_general | solution.py:30
  79.3 1.6 convolution_convert_fusion.1
  81.0 0.7 broadcast_bitcast_fusion
  81.7 19.2 %all-gather.7.cloned.1.call-done = bf16[16384,41]{0,1:T(8,128)(2,1)} async-done(((bf16[2048,41]{0,1:T(8,128)(2,1)}), bf16[16384,41]{0,1:T(8,128)(2,1)}) %all-gather.7.cloned.1.call-update) | async-done | bytes 1343504 | tf_op jit(solution)/shard_map/all_gather | solution.py:12
  100.8 2.3 copy.10
  103.1 0.2 fusion.3
  103.3 0.2 pad.2
  103.5 2.0 copy.11
  105.5 27.7 %fusion.32 = (f32[2048]{0:T(1024)S(1)}, f32[41,2048]{1,0:T(8,128)}) fusion(bf16[16384,41]{0,1:T(8,128)(2,1)} %bitcast.66, bf16[2048,16384]{1,0:T(8,128)(2,1)} %param.7), kind=kOutput, calls=%fused_computation.52 | convolution fusion | flops 2751545344 | bytes 68796416 | tf_op jit(solution)/shard_map/dot_general | solution.py:33
  133.2 1.1 fusion.11
  134.4 1.3 convert_reduce_fusion
  135.7 1.4 pad_maximum_fusion
  137.1 1.5 copy.12
  138.6 22.2 %psum.21 = f32[2]{0:T(128)S(1)} all-reduce(f32[2]{0:T(128)S(1)} %pad_maximum_fusion), channel_id=1, replica_groups=mesh['nodes'=8] {'nodes'}, use_global_device_ids=true, to_apply=%region_5.6 | all-reduce | flops 2 | bytes 16 | tf_op jit(solution)/shard_map/psum | solution.py:38
  160.8 0.6 fusion.31
  161.3 1.3 convert_divide_fusion
  162.7 26.3 %fusion.1 = f32[16384,41]{0,1:T(8,128)} fusion(bf16[2048,16384]{1,0:T(8,128)(2,1)} %param.7, f32[16384]{0:T(1024)} %bitcast.71, f32[41,2048]{1,0:T(8,128)} %get-tuple-element.13, f32[2048]{0:T(1024)S(1)} %convert_divide_fusion, f32[2048]{0:T(1024)S(1)} %get-tuple-element.7, s32[2048]{0:T(1024)} %param.11), kind=kOutput, calls=%fused_computation.3 | convolution fusion | flops 2752638976 | bytes 70221824 | tf_op jit(solution)/shard_map/dot_general | solution.py:19
  189.0 0.2 reduce-scatter.5.cloned.1.call-start
  189.2 39.1 %reduce-scatter.3.cloned.1.call-done = f32[2048,41]{0,1:T(8,128)} async-done(((f32[16384,41]{0,1:T(8,128)}), f32[2048,41]{0,1:T(8,128)}) %reduce-scatter.3.cloned.1.call-update) | async-done | bytes 335888 | tf_op jit(solution)/shard_map/reduce_scatter | solution.py:21
  228.3 27.4 %fusion = f32[16384,128]{0,1:T(8,128)} fusion(bf16[2048,16384]{1,0:T(8,128)(2,1)} %param.7, f32[16384]{0:T(1024)} %bitcast.72, f32[128,2048]{1,0:T(8,128)S(1)} %fusion.33, f32[2048,41]{0,1:T(8,128)} %reduce-scatter.3.cloned.1.call-done, f32[128,41]{0,1:T(8,128)} %param.10), kind=kOutput, calls=%fused_computation.1 | convolution fusion | flops 8614403072 | bytes 76968448 | tf_op jit(solution)/shard_map/dot_general | solution.py:19
  257.2 61.0 %reduce-scatter.5.cloned.1.call-done = f32[2048,128]{0,1:T(8,128)} async-done(((f32[16384,128]{0,1:T(8,128)}), f32[2048,128]{0,1:T(8,128)}) %reduce-scatter.5.cloned.1.call-update) | async-done | bytes 1048592 | tf_op jit(solution)/shard_map/reduce_scatter | solution.py:21
  318.2 2.8 convolution_bitcast_fusion
  321.0 1.9 fusion.16
  322.9 22.8 %psum.23 = f32[128,41]{0,1:T(8,128)} all-reduce(f32[128,41]{0,1:T(8,128)} %fusion.16), channel_id=1, replica_groups=mesh['nodes'=8] {'nodes'}, use_global_device_ids=true, to_apply=%region_9.10 | all-reduce | flops 5248 | bytes 41984 | tf_op jit(solution)/shard_map/psum | solution.py:44
  345.7 18.8 %all-reduce.2.cloned.1.call-done = f32[602,128]{1,0:T(8,128)} async-done(((f32[602,128]{1,0:T(8,128)}), f32[602,128]{1,0:T(8,128)}) %all-reduce.2.cloned.1.call-update) | async-done | bytes 308240 | tf_op jit(solution)/shard_map/psum | solution.py:48
  364.5 1.7 copy.14
  (14 shorter events, 0.2 us)
Async XLA Ops:
  7.2 1.7 copy-start
  7.2 38.1 %all-gather.5.cloned.1.call-start = ((), (), s32[]{:S(2)}) async-start(), calls=%async_computation.5 | async-start | bytes 4718592 | tf_op jit(solution)/shard_map/all_gather | solution.py:12
  11.6 89.3 %all-gather.7.cloned.1.call-start = ((), (), s32[]{:S(2)}) async-start(), calls=%async_computation.6 | async-start | bytes 1769472 | tf_op jit(solution)/shard_map/all_gather | solution.py:12
  80.9 147.4 %reduce-scatter.3.cloned.1.call-start = ((), (), s32[]{:S(2)}) async-start(), calls=%async_computation.2 | async-start | bytes 3538944 | tf_op jit(solution)/shard_map/reduce_scatter | solution.py:21
  105.5 27.7 %copy-start.1 = (s32[2048]{0:T(1024)S(1)}, s32[2048]{0:T(1024)}, u32[]{:S(2)}) copy-start(s32[2048]{0:T(1024)} %param.11) | copy-start | bytes 24580
  133.2 1.1 copy-start.2
  189.0 129.2 %reduce-scatter.5.cloned.1.call-start = ((), (), s32[]{:S(2)}) async-start(), calls=%async_computation.3 | async-start | bytes 9437184 | tf_op jit(solution)/shard_map/reduce_scatter | solution.py:21
  255.8 108.8 %all-reduce.2.cloned.1.call-start = ((), (), s32[]{:S(2)}) async-start(), calls=%async_computation.4 | async-start | bytes 622592 | tf_op jit(solution)/shard_map/psum | solution.py:48
Sparse Core Ops, SparseCore 0:
  11.7 33.5 all-gather.4
  81.1 19.7 all-gather.6
  189.1 39.2 reduce-scatter.2
  255.9 62.2 reduce-scatter.4
  321.7 42.8 all-reduce.1
where the time goes:
time: 375 us; the launch traced here: 374 us
  waiting for transfers between devices  171 us (46%)
  matrix products  120 us (32%)
  blocking collectives  45 us (12%)
  between operations  16.3 us (4%)
  local copies, waits for them, and re-layouts  10.6 us (3%)
  other arithmetic  10.5 us (3%)
    reduce_scatter x2, waiting for transfers between devices, transpose_product_scatter(): lax.psum_scatter(contrib.reshape(-1, width), AXIS_NAME, scatter_dimension...  100 us
    dot_general x2, matrix products, transpose_product_scatter(): lax.dot_general(adj_rows, local_grad, ROW_CONTRACT, preferred_element_typ...  53.7 us
    all_gather x2, waiting for transfers between devices, gather_masked(): gathered = lax.all_gather(local_vals, AXIS_NAME, axis=0, tiled=False)  52.1 us
    dot_general x1, matrix products, device_step(): jnp.dot(adj_rows, gather_masked(proj_one, mask_row), preferred_element_ty...  29.5 us
    dot_general x1, matrix products, device_step(): jnp.dot(adj_rows, gather_masked(proj_two, mask_row), preferred_element_ty...  27.7 us
    psum x1, blocking collectives, device_step(): lax.psum(lax.dot_general(hidden, grad_proj_two, ROW_CONTRACT, preferred_e...  22.8 us
    psum x1, blocking collectives, device_step(): lax.psum(jnp.stack([jnp.sum(label_weight), jnp.sum(label_weight * (log_no...  22.2 us
    psum x1, waiting for transfers between devices, device_step(): lax.psum(lax.dot_general(feat_rows, grad_proj_one, ROW_CONTRACT, preferre...  18.8 us
  transfers between devices with their start and end apart: 5, of which 5 were waited for; matrix products, arithmetic and copies ran while one was open for 1% of the time, Pallas kernels for 0%

commit v1 on v0

v1 whole, which is shorter than its diff:
```python
import jax
import jax.numpy as jnp
from jax import lax
from jax.experimental import pallas as pl
from jax.experimental.pallas import tpu as pltpu
from jax.sharding import PartitionSpec as P

AXIS_NAME = 'nodes'
MESH = pl.DeviceIdType.MESH
F32, BF16 = jnp.float32, jnp.bfloat16
DEVICES = 8
ROWS = 2048
NODES = DEVICES * ROWS
F_IN = 602
F_PAD = 640
HID = 128
CLASSES = 41
C_PAD = 48
HALF = ROWS // 2
SLOTS = 6
CHUNKS = NODES // HALF
SLICE = HID // DEVICES
NT = (((1,), (1,)), ((), ()))


def step_kernel(adj, feat, wh, wo, labels, mask, block_mask, loss_out, gwh_out, gwo_out,
                abuf, xbuf, acc, yall, y2all, ymask, hid, z1t, z2t, wot, lhs1, lhs2, cnt,
                pa, ra, fa, ia, pb, rb, fb, ib, lossall, gwoall, gpart, garr, gred, gfull,
                asem, xsem, ssem, rsem):
    me = lax.axis_index(AXIS_NAME)
    bits = (lax.rem(me, 2), lax.rem(me // 2, 2), me // 4)

    def partner(k):
        return lax.rem(bits[0] + k, 2) + 2 * lax.rem(bits[1] + k // 2, 2) + 4 * lax.rem(bits[2] + k // 4, 2)

    peers = [partner(k) for k in range(DEVICES)]

    def block_half(g):
        back = g // (2 * CHUNKS)
        c = lax.rem(g, CHUNKS)
        k = back * (DEVICES - 1 - c // 2) + (1 - back) * (c // 2)
        return k, lax.rem(c, 2)

    def fetch(g):
        k, h = block_half(g)
        col = pl.multiple_of(partner(k) * ROWS + h * HALF, HALF)
        slot = lax.rem(g, SLOTS)
        return pltpu.make_async_copy(adj.at[:, pl.ds(col, HALF)], abuf.at[slot], asem.at[slot])

    def remote(i, src, dst, k):
        return pltpu.make_async_remote_copy(src_ref=src, dst_ref=dst, send_sem=ssem.at[i], recv_sem=rsem.at[i],
                                            device_id=(peers[k],), device_id_type=MESH)

    for g in range(SLOTS):
        fetch(jnp.int32(g)).start()
    xcopy = pltpu.make_async_copy(feat, xbuf, xsem.at[0])
    xcopy.start()
    barrier = pltpu.get_barrier_semaphore()
    for k in range(1, DEVICES):
        pl.semaphore_signal(barrier, inc=1, device_id=(peers[k],), device_id_type=MESH)

    wot[...] = jnp.zeros_like(wot)
    wot[:, :CLASSES] = wo[...]
    wo_pad = wot[...]
    wot_bf = wo_pad.T[:C_PAD].astype(BF16)
    wo_bf = wo_pad[:, :C_PAD].astype(BF16)
    weight = mask[...].astype(F32)
    cnt[0] = jnp.broadcast_to(jnp.sum(weight, axis=1, keepdims=True), (8, 128))
    xcopy.wait()
    wh_bf = wh[...].astype(BF16)
    yall[0] = jnp.dot(xbuf[...], wh_bf, preferred_element_type=F32).astype(BF16)
    pl.semaphore_wait(barrier, DEVICES - 1)

    def gather_copies(base, y, half):
        h0, h1 = 0, 1
        return [
            remote(base + 0, y.at[0], y.at[1], 1),
            remote(base + 1, half(y, 0, h0), half(y, 2, h0), 2),
            remote(base + 2, half(y, 0, h1), half(y, 2, h1), 2),
            remote(base + 3, half(y, 0, h1), half(y, 4, h1), 4),
            remote(base + 4, half(y, 0, h0), half(y, 4, h0), 4),
            remote(base + 5, half(y, 2, h0), half(y, 3, h0), 1),
            remote(base + 6, half(y, 2, h1), half(y, 3, h1), 1),
            remote(base + 7, half(y, 4, h0), half(y, 5, h0), 1),
            remote(base + 8, half(y, 4, h1), half(y, 5, h1), 1),
            remote(base + 9, half(y, 2, h0), half(y, 6, h0), 4),
            remote(base + 10, half(y, 4, h1), half(y, 6, h1), 2),
            remote(base + 11, half(y, 6, h0), half(y, 7, h0), 1),
            remote(base + 12, half(y, 6, h1), half(y, 7, h1), 1),
        ]

    def row_half(y, slot, h):
        return y.at[slot, pl.ds(h * HALF, HALF), :]

    def col_half(y, slot, h):
        return y.at[slot, :, pl.ds(h * HALF, HALF)]

    def gather_events(copies, c):
        def events(at, waits, starts):
            @pl.when(c == at)
            def _():
                for w in waits:
                    copies[w].wait_recv()
                for s in starts:
                    copies[s].start()
        events(2, (0,), ())
        events(4, (1,), (9, 5))
        events(4, (3,), (10, 8))
        events(5, (2, 4), (6, 7))
        events(6, (5, 6), ())
        events(10, (8, 7), ())
        events(12, (9,), (11,))
        events(12, (10,), (12,))
        events(14, (11, 12), ())

    def mask_value(k):
        return block_mask[me, partner(k)].astype(F32)

    def next_fetch(g):
        @pl.when(g + SLOTS < 4 * CHUNKS)
        def _():
            fetch(g + SLOTS).start()

    copies = gather_copies(0, yall, row_half)
    for i in range(5):
        copies[i].start()
    count_copies = [remote(13 + k, cnt.at[0], cnt.at[k], k) for k in range(1, DEVICES)]
    for copy in count_copies:
        copy.start()
    acc[...] = jnp.zeros_like(acc)

    def pass1(c, carry):
        gather_events(copies, c)
        k, h = block_half(c)
        rows = pl.ds(pl.multiple_of(h * HALF, HALF), HALF)
        ymask[...] = (yall[k, rows, :].astype(F32) * mask_value(k)).astype(BF16)
        fetch(c).wait()
        acc[...] += jnp.dot(abuf[lax.rem(c, SLOTS)], ymask[...], preferred_element_type=F32)
        next_fetch(c)
        return carry
    lax.fori_loop(0, CHUNKS, pass1, 0)

    hid[...] = jnp.maximum(acc[...], 0.0).astype(BF16)
    y2all[0] = lax.dot_general(wot_bf, hid[...], NT, preferred_element_type=F32).astype(BF16)
    for copy in copies + count_copies:
        copy.wait_send()

    copies2 = gather_copies(21, y2all, col_half)
    for i in range(5):
        copies2[i].start()

    def turn(i, carry):
        at = pl.ds(pl.multiple_of(i * 128, 128), 128)
        z1t[:, at] = acc[at, :].T
        return carry
    lax.fori_loop(0, ROWS // 128, turn, 0)
    acc[...] = jnp.zeros_like(acc)

    def pass2(c, carry):
        gather_events(copies2, c)
        k, h = block_half(c)
        cols = pl.ds(pl.multiple_of(h * HALF, HALF), HALF)
        y2mask = (y2all[k, :, cols].astype(F32) * mask_value(k)).astype(BF16)
        g = c + CHUNKS
        fetch(g).wait()
        acc[:, :C_PAD] += lax.dot_general(abuf[lax.rem(g, SLOTS)], y2mask, NT, preferred_element_type=F32)
        next_fetch(g)
        return carry
    lax.fori_loop(0, CHUNKS, pass2, 0)
    for copy in copies2:
        copy.wait_send()

    def turn2(i, carry):
        at = pl.ds(pl.multiple_of(i * 128, 128), 128)
        z2t[:, at] = acc[at, :].T[:C_PAD]
        return carry
    lax.fori_loop(0, ROWS // 128, turn2, 0)
    for copy in count_copies:
        copy.wait_recv()
    label_count = cnt[0, 0:1, 0:1]
    for k in range(1, DEVICES):
        label_count = label_count + cnt[k, 0:1, 0:1]
    loss = jnp.zeros((1, 1), F32)
    for q in range(4):
        at = pl.ds(q * 512, 512)
        z = z2t[:, at]
        row = lax.broadcasted_iota(jnp.int32, (C_PAD, 512), 0)
        z = jnp.where(row < CLASSES, z, -jnp.inf)
        top = jnp.max(z, axis=0, keepdims=True)
        log_norm = jnp.log(jnp.sum(jnp.exp(z - top), axis=0, keepdims=True)) + top
        hot = row == labels[:, at]
        picked = jnp.sum(jnp.where(hot, z, 0.0), axis=0, keepdims=True)
        w = mask[:, at].astype(F32)
        loss = loss + jnp.sum(w * (log_norm - picked), axis=1, keepdims=True)
        prob = jnp.exp(z - log_norm)
        lhs1[:, at] = ((prob - hot.astype(F32)) * (w / label_count)).astype(BF16)
    lossall[me] = jnp.broadcast_to(loss, (8, 128))

    def scatter_copies(base, p, r, f, ix):
        h0, h1 = pl.ds(0, HALF), pl.ds(HALF, HALF)
        return [
            remote(base + 0, p.at[7], r.at[3], 1),
            remote(base + 1, p.at[6, :, h0], f.at[0], 2),
            remote(base + 2, p.at[6, :, h1], f.at[1], 4),
            remote(base + 3, p.at[5], r.at[2], 1),
            remote(base + 4, p.at[4, :, h1], ix.at[1, 1], 4),
            remote(base + 5, p.at[3], r.at[1], 1),
            remote(base + 6, p.at[2, :, h0], ix.at[0, 0], 2),
            remote(base + 7, p.at[1], r.at[0], 1),
            remote(base + 8, p.at[4, :, h0], ix.at[1, 0], 4),
            remote(base + 9, p.at[2, :, h1], ix.at[0, 1], 2),
        ]

    def scatter_events(copies, p, r, f, c, pass_on_at):
        h0, h1 = pl.ds(0, HALF), pl.ds(HALF, HALF)

        def join(k, wait):
            copies[wait].wait_recv()
            p[k] = p[k] + r[k // 2]

        @pl.when(c == 1)
        def _():
            copies[0].start()

        @pl.when(c == 3)
        def _():
            join(6, 0)
            copies[1].start()
            copies[2].start()

        @pl.when(c == 5)
        def _():
            copies[3].start()

        @pl.when(c == 7)
        def _():
            join(4, 3)
            copies[4].start()

        @pl.when(c == 9)
        def _():
            copies[5].start()

        @pl.when(c == 11)
        def _():
            join(2, 5)
            copies[6].start()

        @pl.when(c == 13)
        def _():
            copies[7].start()

        @pl.when(c == pass_on_at)
        def _():
            copies[1].wait_recv()
            p[4, :, h0] = p[4, :, h0] + f[0]
            copies[8].start()
            copies[2].wait_recv()
            p[2, :, h1] = p[2, :, h1] + f[1]
            copies[9].start()

        @pl.when(c == CHUNKS - 1)
        def _():
            join(0, 7)

    def scatter_result(copies, p, ix, h):
        at = pl.ds(h * HALF, HALF)
        return (p[0, :, at] + ix[0, h] + ix[1, h]).astype(BF16)

    copies3 = scatter_copies(34, pa, ra, fa, ia)

    def pass3(c, carry):
        g = c + 2 * CHUNKS
        k, h = block_half(g)
        cols = pl.ds(pl.multiple_of(h * HALF, HALF), HALF)
        fetch(g).wait()
        part = jnp.dot(lhs1[...], abuf[lax.rem(g, SLOTS)], preferred_element_type=F32)
        pa[k, :, cols] = part * mask_value(k)
        next_fetch(g)
        scatter_events(copies3, pa, ra, fa, c, 11)
        return carry
    lax.fori_loop(0, CHUNKS, pass3, 0)
    for i in (6, 9, 4, 8):
        copies3[i].wait_recv()
    for copy in copies3:
        copy.wait_send()
    d2t = jnp.concatenate([scatter_result(copies3, pa, ia, h) for h in range(2)], axis=1)
    gwoall[me] = jnp.dot(d2t, hid[...], preferred_element_type=F32)
    back = jnp.dot(wo_bf, d2t, preferred_element_type=F32)
    lhs2[...] = jnp.where(z1t[...] > 0.0, back, 0.0).astype(BF16)

    small_copies = []
    for k in range(1, DEVICES):
        small_copies.append((remote(44 + k, lossall.at[me], lossall.at[me], k), remote(52 + k, gwoall.at[me], gwoall.at[me], k)))
    for pair in small_copies:
        for copy in pair:
            copy.start()

    copies4 = scatter_copies(60, pb, rb, fb, ib)

    def pass4(c, carry):
        g = c + 3 * CHUNKS
        k, h = block_half(g)
        cols = pl.ds(pl.multiple_of(h * HALF, HALF), HALF)
        fetch(g).wait()
        part = jnp.dot(lhs2[...], abuf[lax.rem(g, SLOTS)], preferred_element_type=F32)
        pb[k, :, cols] = part * mask_value(k)
        next_fetch(g)
        scatter_events(copies4, pb, rb, fb, c, CHUNKS - 1)
        return carry
    lax.fori_loop(0, CHUNKS, pass4, 0)

    for pair in small_copies:
        for copy in pair:
            copy.wait()
    loss = lossall[0, 0:1, 0:1]
    gwo = gwoall[0]
    for d in range(1, DEVICES):
        loss = loss + lossall[d, 0:1, 0:1]
        gwo = gwo + gwoall[d]
    loss_out[...] = loss / label_count
    wot[...] = jnp.zeros_like(wot)
    wot[:C_PAD, :] = gwo
    gwo_out[...] = wot[...].T[:, :CLASSES]

    for i in (6, 9, 4, 8):
        copies4[i].wait_recv()
    for copy in copies4:
        copy.wait_send()
    d1t = jnp.concatenate([scatter_result(copies4, pb, ib, h) for h in range(2)], axis=1)
    gpart[:, :F_IN] = jnp.dot(d1t, xbuf[...], preferred_element_type=F32)

    mine = pl.ds(pl.multiple_of(me * SLICE, SLICE), SLICE)
    parts = []
    for k in range(1, DEVICES):
        theirs = pl.ds(pl.multiple_of(peers[k] * SLICE, SLICE), SLICE)
        parts.append(remote(70 + k, gpart.at[theirs, :], garr.at[me], k))
    for copy in parts:
        copy.start()
    garr[me] = gpart[mine, :]
    for copy in parts:
        copy.wait()
    total = garr[0]
    for d in range(1, DEVICES):
        total = total + garr[d]
    gred[...] = total
    wholes = [remote(78 + k, gred, gfull.at[mine, :], k) for k in range(1, DEVICES)]
    for copy in wholes:
        copy.start()
    gfull[mine, :] = total
    for copy in wholes:
        copy.wait()
    for i in range(F_PAD // 128):
        at = pl.ds(i * 128, 128)
        n = min(128, F_IN - i * 128)
        gwh_out[i * 128:i * 128 + n, :] = gfull[:, at].T[:n]


def device_step(adj, feat, w_hidden, w_output, labels, train_mask, block_mask):
    vmem = pl.BlockSpec(memory_space=pltpu.VMEM)
    hbm = pl.BlockSpec(memory_space=pl.ANY)
    v = pltpu.VMEM
    copies = 86
    loss, gwh, gwo = pl.pallas_call(
        step_kernel,
        out_shape=(jax.ShapeDtypeStruct((1, 1), F32), jax.ShapeDtypeStruct((F_IN, HID), F32), jax.ShapeDtypeStruct((HID, CLASSES), F32)),
        in_specs=[hbm, hbm, vmem, vmem, vmem, vmem, pl.BlockSpec(memory_space=pltpu.SMEM)],
        out_specs=(vmem, vmem, vmem),
        scratch_shapes=[
            v((SLOTS, ROWS, HALF), BF16), v((ROWS, F_IN), BF16), v((ROWS, HID), F32),
            v((DEVICES, ROWS, HID), BF16), v((DEVICES, C_PAD, ROWS), BF16), v((HALF, HID), BF16), v((ROWS, HID), BF16),
            v((HID, ROWS), F32), v((C_PAD, ROWS), F32), v((128, 128), F32), v((C_PAD, ROWS), BF16), v((HID, ROWS), BF16),
            v((DEVICES, 8, 128), F32),
            v((DEVICES, C_PAD, ROWS), F32), v((4, C_PAD, ROWS), F32), v((2, C_PAD, HALF), F32), v((2, 2, C_PAD, HALF), F32),
            v((DEVICES, HID, ROWS), F32), v((4, HID, ROWS), F32), v((2, HID, HALF), F32), v((2, 2, HID, HALF), F32),
            v((DEVICES, 8, 128), F32), v((DEVICES, C_PAD, HID), F32),
            v((HID, F_PAD), F32), v((DEVICES, SLICE, F_PAD), F32), v((SLICE, F_PAD), F32), v((HID, F_PAD), F32),
            pltpu.SemaphoreType.DMA((SLOTS,)), pltpu.SemaphoreType.DMA((1,)),
            pltpu.SemaphoreType.DMA((copies,)), pltpu.SemaphoreType.DMA((copies,)),
        ],
        compiler_params=pltpu.CompilerParams(collective_id=0, has_side_effects=True, vmem_limit_bytes=67043328),
        name='gcn_step',
    )(adj, feat, w_hidden, w_output, labels.reshape(1, ROWS), train_mask.reshape(1, ROWS), block_mask)
    return loss[0, 0], gwh, gwo


def solution(mesh):
    row_spec = P(AXIS_NAME, None)
    vec_spec = P(AXIS_NAME)
    return jax.shard_map(device_step, mesh=mesh, in_specs=(row_spec, row_spec, P(), P(), vec_spec, vec_spec, P()), out_specs=(P(), P(), P()), check_vma=False)
```

time: 375 us -> 154 us (0.41)
  waiting for transfers between devices: 171 us -> 0 us
  Pallas kernels: 0 us -> 142 us
  matrix products: 120 us -> 0 us
  blocking collectives: 45 us -> 0 us
  between operations: 16.3 us -> 2.39 us
  other arithmetic: 10.5 us -> 0 us
    pallas_call x0 -> x1, Pallas kernels: none -> 142 us  [device_step(): pl.pallas_call(step_kernel, out_shape=(jax.ShapeDtypeStruct((1, 1), F32),...]
    dot_general x8 -> x0, matrix products: 120 us -> none  [the longest x2 53.7 us: transpose_product_scatter(): lax.dot_general(adj_rows, local_grad, ROW_CONTRACT, preferred_element_typ...]
    reduce_scatter x2 -> x0, waiting for transfers between devices: 100 us -> none  [transpose_product_scatter(): lax.psum_scatter(contrib.reshape(-1, width), AXIS_NAME, scatter_dimension...]
    all_gather x2 -> x0, waiting for transfers between devices: 52.1 us -> none  [gather_masked(): gathered = lax.all_gather(local_vals, AXIS_NAME, axis=0, tiled=False)]
    psum x2 -> x0, blocking collectives: 45 us -> none  [the longest x1 22.8 us: device_step(): lax.psum(lax.dot_general(hidden, grad_proj_two, ROW_CONTRACT, preferred_e...]
    psum x1 -> x0, waiting for transfers between devices: 18.8 us -> none  [device_step(): lax.psum(lax.dot_general(feat_rows, grad_proj_one, ROW_CONTRACT, preferre...]
    mul x1 -> x0, other arithmetic: 4.5 us -> none  [gather_masked(): gathered = gathered * mask_row.astype(local_vals.dtype)[:, None, None]]
    unnamed x12 -> x4, local copies, waits for them, and re-layouts: 10 us -> 9.07 us
  transfers between devices with their start and end apart: 5 -> 0, of which waited for: 5 -> 0; matrix products, arithmetic and copies ran while one was open for 1% -> 0% of each run, Pallas kernels for 0% -> 0%
where the time goes in v1:
time: 154 us
  Pallas kernels  142 us (92%)
  local copies, waits for them, and re-layouts  9.07 us (6%)
  between operations  2.39 us (2%)
    pallas_call x1, Pallas kernels, device_step(): pl.pallas_call(step_kernel, out_shape=(jax.ShapeDtypeStruct((1, 1), F32),...  142 us
    unnamed x4, local copies, waits for them, and re-layouts  9.07 us

profile of v1, /device:TPU:0, one launch (start us, length us, event | category | flops | bytes accessed | tf_op | source)
XLA Modules:
  0.0 153.8 jit_solution(4173041545527372455)
XLA Ops:
  0.6 1.5 copy.11.wo
  2.1 4.4 %copy.10.feat = bf16[2048,602]{1,0:T(8,128)(2,1)} copy(bf16[2048,602]{0,1:T(8,128)(2,1)} %param.8) | data formatting | bytes 4931584 | tf_op args[1]
  6.5 142.4 %gcn_step.1 = (f32[1,1]{1,0:T(1,128)}, f32[602,128]{1,0:T(8,128)}, f32[128,41]{1,0:T(8,128)}) custom-call(bf16[2048,16384]{1,0:T(8,128)(2,1)} %adj.1, bf16[2048,602]{1,0:T(8,128)(2,1)} %copy.10.feat, f32[602,128]{1,0:T(8,128)} %wh.1, f32[128,41]{1,0:T(8,128)} %copy.11.wo, s32[1,2048]{1,0:T(1,128)} %bitcast.3, s32[1,2048]{1,0:T(1,128)} %bitcast.4, ...), custom_call_target="tpu_custom_call" | custom-call | tf_op jit(solution)/shard_map/gcn_step/pallas_call | solution.py:364
  148.8 1.5 copy.12
  151.0 1.7 %copy.16 = f32[602,128]{1,0:T(8,128)} copy(f32[602,128]{1,0:T(8,128)} %get-tuple-element.16) | data formatting | bytes 616448

commit v2 on v0

v2 whole, which is shorter than its diff:
```python
import jax
import jax.numpy as jnp
from jax import lax
from jax.experimental import pallas as pl
from jax.experimental.pallas import tpu as pltpu
from jax.sharding import PartitionSpec as P

AXIS_NAME = 'nodes'
MESH = pl.DeviceIdType.MESH
F32, BF16 = jnp.float32, jnp.bfloat16
DEVICES = 8
ROWS = 2048
NODES = DEVICES * ROWS
F_IN = 602
HID = 128
CLASSES = 41
C_PAD = 48
HALF = ROWS // 2
QUART = ROWS // 4
SLOTS = 6
CHUNKS = NODES // HALF
SUM_ROWS = 672
GWO_ROW = 608
LOSS_ROW = GWO_ROW + C_PAD
NT = (((1,), (1,)), ((), ()))


def step_kernel(adj, feat, wh, wo, labels, mask, block_mask, loss_out, gwh_out, gwo_out,
                abuf, xbuf, acc, yall, y2all, ymask, hid, z1t, z2t, wpad, lhs1, lhs2, cnt,
                pa, ra, fa, ia, pb, rb, fb, ib, gpart, gpair, gacross, gback,
                asem, xsem, ssem, rsem):
    me = lax.axis_index(AXIS_NAME)
    bits = (lax.rem(me, 2), lax.rem(me // 2, 2), me // 4)

    def partner(k):
        return lax.rem(bits[0] + k, 2) + 2 * lax.rem(bits[1] + k // 2, 2) + 4 * lax.rem(bits[2] + k // 4, 2)

    peers = [partner(k) for k in range(DEVICES)]

    def block_half(g):
        back = g // (2 * CHUNKS)
        c = lax.rem(g, CHUNKS)
        q, r = c // 4, lax.rem(c, 4)
        forth_k = 2 * q + r // 2
        forth_h = lax.rem(r, 2)
        back_k = DEVICES - 1 - 2 * q - lax.rem(r, 2)
        back_h = r // 2
        return back * back_k + (1 - back) * forth_k, back * back_h + (1 - back) * forth_h

    def fetch(g):
        k, h = block_half(g)
        col = pl.multiple_of(partner(k) * ROWS + h * HALF, HALF)
        slot = lax.rem(g, SLOTS)
        return pltpu.make_async_copy(adj.at[:, pl.ds(col, HALF)], abuf.at[slot], asem.at[slot])

    used = [0]

    def remote(src, dst, k):
        i = used[0]
        used[0] += 1
        return pltpu.make_async_remote_copy(src_ref=src, dst_ref=dst, send_sem=ssem.at[i], recv_sem=rsem.at[i],
                                            device_id=(peers[k],), device_id_type=MESH)

    xcopy = pltpu.make_async_copy(feat, xbuf, xsem.at[0])
    xcopy.start()
    for g in range(SLOTS):
        fetch(jnp.int32(g)).start()
    barrier = pltpu.get_barrier_semaphore()
    for k in range(1, DEVICES):
        pl.semaphore_signal(barrier, inc=1, device_id=(peers[k],), device_id_type=MESH)

    wpad[...] = jnp.zeros_like(wpad)
    wpad[:CLASSES, :] = wo[...]
    wot_bf = wpad[:C_PAD, :].astype(BF16)
    wo_bf = wpad[...].T[:, :C_PAD].astype(BF16)
    wh_t = wh[...].T.astype(BF16)
    weight = mask[...].astype(F32)
    cnt[0] = jnp.broadcast_to(jnp.sum(weight, axis=1, keepdims=True), (8, 128))
    xcopy.wait()
    yall[0] = jnp.dot(wh_t, xbuf[...], preferred_element_type=F32).astype(BF16)
    pl.semaphore_wait(barrier, DEVICES - 1)

    def gather_copies(y):
        def half(k, h):
            return y.at[k, :, pl.ds(h * HALF, HALF)]

        def quart(k, q):
            return y.at[k, :, pl.ds(q * QUART, QUART)]

        copies = {'own': remote(y.at[0], y.at[1], 1)}
        for h in range(2):
            copies['x', h] = remote(half(0, h), half(2, h), 2)
            copies['y', h] = remote(half(0, h), half(4, h), 4)
            copies['x core', h] = remote(half(2, h), half(3, h), 1)
            copies['y core', h] = remote(half(4, h), half(5, h), 1)
            copies['xy', h] = remote(quart(2, 2 * h), quart(6, 2 * h), 4)
            copies['yx', h] = remote(quart(4, 2 * h + 1), quart(6, 2 * h + 1), 2)
            copies['xy core', h] = remote(half(6, h), half(7, h), 1)
        return copies

    def gather_start(copies):
        for name in (('x', 0), ('y', 0), ('x', 1), ('y', 1), 'own'):
            copies[name].start()

    def gather_events(copies, c):
        @pl.when(c == 2)
        def _():
            copies['own'].wait_recv()

        for h in range(2):
            @pl.when(c == 4 + h)
            def _(h=h):
                copies['x', h].wait_recv()
                copies['xy', h].start()
                copies['x core', h].start()
                copies['y', h].wait_recv()
                copies['yx', h].start()
                copies['y core', h].start()

            @pl.when(c == 6 + h)
            def _(h=h):
                copies['x core', h].wait_recv()

            @pl.when(c == 10 + h)
            def _(h=h):
                copies['y core', h].wait_recv()

            @pl.when(c == 12 + h)
            def _(h=h):
                copies['xy', h].wait_recv()
                copies['yx', h].wait_recv()
                copies['xy core', h].start()

            @pl.when(c == 14 + h)
            def _(h=h):
                copies['xy core', h].wait_recv()

    def mask_value(k):
        return block_mask[me, partner(k)].astype(F32)

    def next_fetch(g):
        @pl.when(g + SLOTS < 4 * CHUNKS)
        def _():
            fetch(g + SLOTS).start()

    def masked(y, k, h):
        cols = pl.ds(pl.multiple_of(h * HALF, HALF), HALF)
        return (y[k, :, cols].astype(F32) * mask_value(k)).astype(BF16)

    copies1 = gather_copies(yall)
    gather_start(copies1)
    acc[...] = jnp.zeros_like(acc)

    def pass1(c, carry):
        gather_events(copies1, c)
        k, h = block_half(c)
        ymask[...] = masked(yall, k, h)
        fetch(c).wait()
        acc[...] += lax.dot_general(abuf[lax.rem(c, SLOTS)], ymask[...], NT, preferred_element_type=F32)
        next_fetch(c)
        return carry
    lax.fori_loop(0, CHUNKS, pass1, 0)

    hid[...] = jnp.maximum(acc[...], 0.0).astype(BF16)
    y2all[0] = lax.dot_general(wot_bf, hid[...], NT, preferred_element_type=F32).astype(BF16)

    copies2 = gather_copies(y2all)
    gather_start(copies2)
    count_copies = [remote(cnt.at[0], cnt.at[k], k) for k in range(1, DEVICES)]
    for copy in count_copies:
        copy.start()
    for copy in copies1.values():
        copy.wait_send()

    def turn(i, carry):
        at = pl.ds(pl.multiple_of(i * 128, 128), 128)
        z1t[:, at] = acc[at, :].T
        return carry
    lax.fori_loop(0, ROWS // 128, turn, 0)
    acc[...] = jnp.zeros_like(acc)

    def pass2(c, carry):
        gather_events(copies2, c)
        k, h = block_half(c)
        ymask[:C_PAD, :] = masked(y2all, k, h)
        g = c + CHUNKS
        fetch(g).wait()
        acc[:, :C_PAD] += lax.dot_general(abuf[lax.rem(g, SLOTS)], ymask[:C_PAD, :], NT, preferred_element_type=F32)
        next_fetch(g)
        return carry
    lax.fori_loop(0, CHUNKS, pass2, 0)

    def turn2(i, carry):
        at = pl.ds(pl.multiple_of(i * 128, 128), 128)
        z2t[:, at] = acc[at, :].T[:C_PAD]
        return carry
    lax.fori_loop(0, ROWS // 128, turn2, 0)
    for copy in count_copies:
        copy.wait_recv()
    label_count = cnt[0, 0:1, 0:1]
    for k in range(1, DEVICES):
        label_count = label_count + cnt[k, 0:1, 0:1]
    loss = jnp.zeros((1, 1), F32)
    for q in range(4):
        at = pl.ds(q * QUART, QUART)
        z = z2t[:, at]
        row = lax.broadcasted_iota(jnp.int32, (C_PAD, QUART), 0)
        z = jnp.where(row < CLASSES, z, -jnp.inf)
        top = jnp.max(z, axis=0, keepdims=True)
        log_norm = jnp.log(jnp.sum(jnp.exp(z - top), axis=0, keepdims=True)) + top
        hot = row == labels[:, at]
        picked = jnp.sum(jnp.where(hot, z, 0.0), axis=0, keepdims=True)
        w = mask[:, at].astype(F32)
        loss = loss + jnp.sum(w * (log_norm - picked), axis=1, keepdims=True)
        prob = jnp.exp(z - log_norm)
        lhs1[:, at] = ((prob - hot.astype(F32)) * (w / label_count)).astype(BF16)

    def scatter_copies(p, r, f, ix):
        def half(k, h):
            return p.at[k, :, pl.ds(h * HALF, HALF)]

        def quart(k, q):
            return p.at[k, :, pl.ds(q * QUART, QUART)]

        copies = {}
        for h in range(2):
            even, odd = 2 * h, 2 * h + 1
            for k in (7, 5, 3, 1):
                copies['core', k, h] = remote(half(k, h), r.at[k // 2, h], 1)
            copies['xy', h] = remote(quart(6, even), f.at[0, h], 2)
            copies['yx', h] = remote(quart(6, odd), f.at[1, h], 4)
            copies['y raw', h] = remote(quart(4, odd), ix.at[1, odd], 4)
            copies['x raw', h] = remote(quart(2, even), ix.at[0, even], 2)
            copies['y', h] = remote(quart(4, even), ix.at[1, even], 4)
            copies['x', h] = remote(quart(2, odd), ix.at[0, odd], 2)
        return copies

    def scatter_events(copies, p, r, f, c, pass_on):
        sends = {6: ('xy', 'yx'), 4: ('y raw',), 2: ('x raw',), 0: ()}
        for q in range(4):
            for h in range(2):
                k = 6 - 2 * q

                @pl.when(c == 4 * q + 2 * h)
                def _(k=k, h=h):
                    copies['core', k + 1, h].start()

                @pl.when(c == 4 * q + 2 * h + 1)
                def _(k=k, h=h):
                    at = pl.ds(h * HALF, HALF)
                    copies['core', k + 1, h].wait_recv()
                    p[k, :, at] = p[k, :, at] + r[k // 2, h]
                    for name in sends[k]:
                        copies[name, h].start()

        for h in range(2):
            @pl.when(c == pass_on[h])
            def _(h=h):
                even, odd = pl.ds(2 * h * QUART, QUART), pl.ds((2 * h + 1) * QUART, QUART)
                copies['xy', h].wait_recv()
                p[4, :, even] = p[4, :, even] + f[0, h]
                copies['y', h].start()
                copies['yx', h].wait_recv()
                p[2, :, odd] = p[2, :, odd] + f[1, h]
                copies['x', h].start()

    def scatter_result(copies, p, ix, q):
        h = q // 2
        for name in (('y', 'x raw') if q % 2 == 0 else ('y raw', 'x')):
            copies[name, h].wait_recv()
        return (p[0, :, pl.ds(q * QUART, QUART)] + ix[0, q] + ix[1, q]).astype(BF16)

    copies3 = scatter_copies(pa, ra, fa, ia)

    def pass3(c, carry):
        g = c + 2 * CHUNKS
        k, h = block_half(g)
        cols = pl.ds(pl.multiple_of(h * HALF, HALF), HALF)
        fetch(g).wait()
        part = jnp.dot(lhs1[...], abuf[lax.rem(g, SLOTS)], preferred_element_type=F32)
        pa[k, :, cols] = part * mask_value(k)
        next_fetch(g)
        scatter_events(copies3, pa, ra, fa, c, (11, 11))
        return carry
    lax.fori_loop(0, CHUNKS, pass3, 0)
    d2t = jnp.concatenate([scatter_result(copies3, pa, ia, q) for q in range(4)], axis=1)
    back = jnp.dot(wo_bf, d2t, preferred_element_type=F32)
    lhs2[...] = jnp.where(z1t[...] > 0.0, back, 0.0).astype(BF16)

    copies4 = scatter_copies(pb, rb, fb, ib)

    def pass4(c, carry):
        g = c + 3 * CHUNKS
        k, h = block_half(g)
        cols = pl.ds(pl.multiple_of(h * HALF, HALF), HALF)
        fetch(g).wait()
        part = jnp.dot(lhs2[...], abuf[lax.rem(g, SLOTS)], preferred_element_type=F32)
        pb[k, :, cols] = part * mask_value(k)
        next_fetch(g)
        scatter_events(copies4, pb, rb, fb, c, (11, 13))
        return carry
    lax.fori_loop(0, CHUNKS, pass4, 0)

    gpart[F_IN // 8 * 8:GWO_ROW, :] = jnp.zeros((8, HID), F32)
    gpart[GWO_ROW:LOSS_ROW, :] = jnp.dot(d2t, hid[...], preferred_element_type=F32)
    gpart[LOSS_ROW:SUM_ROWS, :] = jnp.broadcast_to(loss / label_count, (SUM_ROWS - LOSS_ROW, HID))
    for copy in list(copies2.values()) + count_copies + list(copies3.values()):
        copy.wait_send()
    for q in range(4):
        term = lax.dot_general(xbuf[:, q * QUART:(q + 1) * QUART], scatter_result(copies4, pb, ib, q), NT, preferred_element_type=F32)
        if q == 0:
            gpart[:F_IN, :] = term
        else:
            gpart[:F_IN, :] += term

    half_rows, quart_rows = SUM_ROWS // 2, SUM_ROWS // 4
    mine = pl.ds(pl.multiple_of(bits[0] * half_rows, 8), half_rows)
    other = pl.ds(pl.multiple_of((1 - bits[0]) * half_rows, 8), half_rows)
    swap = remote(gpart.at[other, :], gpair, 1)
    swap.start()
    swap.wait()
    gpart[mine, :] = gpart[mine, :] + gpair[...]
    quarts = [pl.ds(pl.multiple_of(bits[0] * half_rows + q * quart_rows, 8), quart_rows) for q in range(2)]
    for step, ways in enumerate(((2, 4), (4, 2))):
        copies = [remote(gpart.at[quarts[q], :], gacross.at[step, q], ways[q]) for q in range(2)]
        for copy in copies:
            copy.start()
        for q in range(2):
            copies[q].wait()
            gpart[quarts[q], :] = gpart[quarts[q], :] + gacross[step, q]
    final = remote(gpart.at[mine, :], gback, 1)
    final.start()
    for copy in copies4.values():
        copy.wait_send()
    final.wait()
    gpart[other, :] = gback[...]
    gwh_out[...] = gpart[:F_IN, :]
    gwo_out[...] = gpart[GWO_ROW:GWO_ROW + CLASSES, :]
    loss_out[...] = gpart[LOSS_ROW:LOSS_ROW + 1, 0:1]


def device_step(adj, feat, w_hidden, w_output, labels, train_mask, block_mask):
    vmem = pl.BlockSpec(memory_space=pltpu.VMEM)
    hbm = pl.BlockSpec(memory_space=pl.ANY)
    v = pltpu.VMEM
    copies = 96
    loss, gwh, gwo = pl.pallas_call(
        step_kernel,
        out_shape=(jax.ShapeDtypeStruct((1, 1), F32), jax.ShapeDtypeStruct((F_IN, HID), F32), jax.ShapeDtypeStruct((CLASSES, HID), F32)),
        in_specs=[hbm, hbm, vmem, vmem, vmem, vmem, pl.BlockSpec(memory_space=pltpu.SMEM)],
        out_specs=(vmem, vmem, vmem),
        scratch_shapes=[
            v((SLOTS, ROWS, HALF), BF16), v((F_IN, ROWS), BF16), v((ROWS, HID), F32),
            v((DEVICES, HID, ROWS), BF16), v((DEVICES, C_PAD, ROWS), BF16), v((HID, HALF), BF16), v((ROWS, HID), BF16),
            v((HID, ROWS), F32), v((C_PAD, ROWS), F32), v((128, 128), F32), v((C_PAD, ROWS), BF16), v((HID, ROWS), BF16),
            v((DEVICES, 8, 128), F32),
            v((DEVICES, C_PAD, ROWS), F32), v((4, 2, C_PAD, HALF), F32), v((2, 2, C_PAD, QUART), F32), v((2, 4, C_PAD, QUART), F32),
            v((DEVICES, HID, ROWS), F32), v((4, 2, HID, HALF), F32), v((2, 2, HID, QUART), F32), v((2, 4, HID, QUART), F32),
            v((SUM_ROWS, HID), F32), v((SUM_ROWS // 2, HID), F32), v((2, 2, SUM_ROWS // 4, HID), F32), v((SUM_ROWS // 2, HID), F32),
            pltpu.SemaphoreType.DMA((SLOTS,)), pltpu.SemaphoreType.DMA((1,)),
            pltpu.SemaphoreType.DMA((copies,)), pltpu.SemaphoreType.DMA((copies,)),
        ],
        compiler_params=pltpu.CompilerParams(collective_id=0, has_side_effects=True, vmem_limit_bytes=67043328),
        name='gcn_step',
    )(adj, feat.T, w_hidden, w_output.T, labels.reshape(1, ROWS), train_mask.reshape(1, ROWS), block_mask)
    return loss[0, 0], gwh, gwo.T


def solution(mesh):
    row_spec = P(AXIS_NAME, None)
    vec_spec = P(AXIS_NAME)
    return jax.shard_map(device_step, mesh=mesh, in_specs=(row_spec, row_spec, P(), P(), vec_spec, vec_spec, P()), out_specs=(P(), P(), P()), check_vma=False)
```

time: 375 us -> 145 us (0.39)
  waiting for transfers between devices: 171 us -> 0 us
  Pallas kernels: 0 us -> 139 us
  matrix products: 120 us -> 0 us
  blocking collectives: 45 us -> 0 us
  between operations: 16.3 us -> 2.39 us
  other arithmetic: 10.5 us -> 0 us
  local copies, waits for them, and re-layouts: 10.6 us -> 3.05 us
    pallas_call x0 -> x1, Pallas kernels: none -> 139 us  [device_step(): pl.pallas_call(step_kernel, out_shape=(jax.ShapeDtypeStruct((1, 1), F32),...]
    dot_general x8 -> x0, matrix products: 120 us -> none  [the longest x2 53.7 us: transpose_product_scatter(): lax.dot_general(adj_rows, local_grad, ROW_CONTRACT, preferred_element_typ...]
    reduce_scatter x2 -> x0, waiting for transfers between devices: 100 us -> none  [transpose_product_scatter(): lax.psum_scatter(contrib.reshape(-1, width), AXIS_NAME, scatter_dimension...]
    all_gather x2 -> x0, waiting for transfers between devices: 52.1 us -> none  [gather_masked(): gathered = lax.all_gather(local_vals, AXIS_NAME, axis=0, tiled=False)]
    psum x2 -> x0, blocking collectives: 45 us -> none  [the longest x1 22.8 us: device_step(): lax.psum(lax.dot_general(hidden, grad_proj_two, ROW_CONTRACT, preferred_e...]
    psum x1 -> x0, waiting for transfers between devices: 18.8 us -> none  [device_step(): lax.psum(lax.dot_general(feat_rows, grad_proj_one, ROW_CONTRACT, preferre...]
    unnamed x12 -> x2, local copies, waits for them, and re-layouts: 10 us -> 3.05 us
    mul x1 -> x0, other arithmetic: 4.5 us -> none  [gather_masked(): gathered = gathered * mask_row.astype(local_vals.dtype)[:, None, None]]
  transfers between devices with their start and end apart: 5 -> 0, of which waited for: 5 -> 0; matrix products, arithmetic and copies ran while one was open for 1% -> 0% of each run, Pallas kernels for 0% -> 0%
where the time goes in v2:
time: 145 us
  Pallas kernels  139 us (96%)
  local copies, waits for them, and re-layouts  3.05 us (2%)
  between operations  2.39 us (2%)
    pallas_call x1, Pallas kernels, device_step(): pl.pallas_call(step_kernel, out_shape=(jax.ShapeDtypeStruct((1, 1), F32),...  139 us
    unnamed x2, local copies, waits for them, and re-layouts  3.05 us

profile of v2, /device:TPU:0, one launch (start us, length us, event | category | flops | bytes accessed | tf_op | source)
XLA Modules:
  0.0 144.9 jit_solution(13074342196674312041)
XLA Ops:
  0.6 139.4 %gcn_step.1 = (f32[1,1]{1,0:T(1,128)}, f32[602,128]{1,0:T(8,128)}, f32[41,128]{1,0:T(8,128)}) custom-call(bf16[2048,16384]{1,0:T(8,128)(2,1)} %adj.1, bf16[602,2048]{1,0:T(8,128)(2,1)} %bitcast.6, f32[602,128]{1,0:T(8,128)} %wh.1, f32[41,128]{1,0:T(8,128)} %bitcast.7, s32[1,2048]{1,0:T(1,128)} %bitcast.9, s32[1,2048]{1,0:T(1,128)} %bitcast.10, s32[8,8]{1,0:T(8,128)} %block_mask.1), custom_call_target="tpu_custom_call" | custom-call | tf_op jit(solution)/shard_map/gcn_step/pallas_call | solution.py:347
  140.7 1.7 %copy.14 = f32[602,128]{1,0:T(8,128)} copy(f32[602,128]{1,0:T(8,128)} %get-tuple-element.13) | data formatting | bytes 616448
  142.4 1.3 copy.15

commit v3 on v2

--- a/solution.py
+++ b/solution.py
@@ -37,21 +37,36 @@
 
     peers = [partner(k) for k in range(DEVICES)]
 
-    def block_half(g):
-        back = g // (2 * CHUNKS)
+    def block_quart(g, i):
+        back = lax.div(g, 2 * CHUNKS)
         c = lax.rem(g, CHUNKS)
-        q, r = c // 4, lax.rem(c, 4)
-        forth_k = 2 * q + r // 2
-        forth_h = lax.rem(r, 2)
-        back_k = DEVICES - 1 - 2 * q - lax.rem(r, 2)
-        back_h = r // 2
-        return back * back_k + (1 - back) * forth_k, back * back_h + (1 - back) * forth_h
-
-    def fetch(g):
-        k, h = block_half(g)
-        col = pl.multiple_of(partner(k) * ROWS + h * HALF, HALF)
-        slot = lax.rem(g, SLOTS)
-        return pltpu.make_async_copy(adj.at[:, pl.ds(col, HALF)], abuf.at[slot], asem.at[slot])
+        q, r = lax.div(c, 4), lax.rem(c, 4)
+        mid = lax.div(q * (3 - q), 2)
+        last = lax.div(q, 3)
+        pair, odd = lax.div(c, 2), lax.rem(c, 2)
+        forth_k = mid * (2 + odd + 2 * i) + (1 - mid) * (last * (6 + odd) + (1 - last) * pair)
+        forth_q = mid * (pair - 2) + (1 - mid) * (2 * (last * (pair - 6) + (1 - last) * odd) + i)
+        back_k, back_h = mid * (5 - r) + (1 - mid) * (7 - 6 * last - odd), mid * (q - 1) + (1 - mid) * lax.div(r, 2)
+        return back * back_k + (1 - back) * forth_k, back * (2 * back_h + i) + (1 - back) * forth_q
+
+    class Fetch:
+        def __init__(self, g):
+            slot = lax.rem(g, SLOTS)
+            self.pieces = []
+            for i in range(2):
+                k, q = block_quart(g, i)
+                col = pl.multiple_of(partner(k) * ROWS + q * QUART, QUART)
+                self.pieces.append(pltpu.make_async_copy(adj.at[:, pl.ds(col, QUART)], abuf.at[slot, :, pl.ds(i * QUART, QUART)], asem.at[slot, i]))
+
+        def start(self):
+            for piece in self.pieces:
+                piece.start()
+
+        def wait(self):
+            for piece in self.pieces:
+                piece.wait()
+
+    fetch = Fetch
 
     used = [0]
 
@@ -63,8 +78,7 @@
 
     xcopy = pltpu.make_async_copy(feat, xbuf, xsem.at[0])
     xcopy.start()
-    for g in range(SLOTS):
-        fetch(jnp.int32(g)).start()
+    fetch(jnp.int32(0)).start()
     barrier = pltpu.get_barrier_semaphore()
     for k in range(1, DEVICES):
         pl.semaphore_signal(barrier, inc=1, device_id=(peers[k],), device_id_type=MESH)
@@ -77,6 +91,8 @@
     weight = mask[...].astype(F32)
     cnt[0] = jnp.broadcast_to(jnp.sum(weight, axis=1, keepdims=True), (8, 128))
     xcopy.wait()
+    for g in range(1, SLOTS):
+        fetch(jnp.int32(g)).start()
     yall[0] = jnp.dot(wh_t, xbuf[...], preferred_element_type=F32).astype(BF16)
     pl.semaphore_wait(barrier, DEVICES - 1)
 
@@ -88,52 +104,51 @@
             return y.at[k, :, pl.ds(q * QUART, QUART)]
 
         copies = {'own': remote(y.at[0], y.at[1], 1)}
+        for q in range(4):
+            copies['x', q] = remote(quart(0, q), quart(2, q), 2)
+            copies['y', q] = remote(quart(0, q), quart(4, q), 4)
+            copies['x core', q] = remote(quart(2, q), quart(3, q), 1)
+            copies['y core', q] = remote(quart(4, q), quart(5, q), 1)
+            if q % 2 == 0:
+                copies['across', q] = remote(quart(2, q), quart(6, q), 4)
+            else:
+                copies['across', q] = remote(quart(4, q), quart(6, q), 2)
         for h in range(2):
-            copies['x', h] = remote(half(0, h), half(2, h), 2)
-            copies['y', h] = remote(half(0, h), half(4, h), 4)
-            copies['x core', h] = remote(half(2, h), half(3, h), 1)
-            copies['y core', h] = remote(half(4, h), half(5, h), 1)
-            copies['xy', h] = remote(quart(2, 2 * h), quart(6, 2 * h), 4)
-            copies['yx', h] = remote(quart(4, 2 * h + 1), quart(6, 2 * h + 1), 2)
-            copies['xy core', h] = remote(half(6, h), half(7, h), 1)
+            copies['across core', h] = remote(half(6, h), half(7, h), 1)
         return copies
 
     def gather_start(copies):
-        for name in (('x', 0), ('y', 0), ('x', 1), ('y', 1), 'own'):
-            copies[name].start()
-
-    def gather_events(copies, c):
-        @pl.when(c == 2)
-        def _():
+        for q in range(4):
+            copies['x', q].start()
+            copies['y', q].start()
+            if q == 0:
+                copies['own'].start()
+
+    def gather_need(copies, c):
+        if c == 2:
             copies['own'].wait_recv()
-
-        for h in range(2):
-            @pl.when(c == 4 + h)
-            def _(h=h):
-                copies['x', h].wait_recv()
-                copies['xy', h].start()
-                copies['x core', h].start()
-                copies['y', h].wait_recv()
-                copies['yx', h].start()
-                copies['y core', h].start()
-
-            @pl.when(c == 6 + h)
-            def _(h=h):
-                copies['x core', h].wait_recv()
-
-            @pl.when(c == 10 + h)
-            def _(h=h):
-                copies['y core', h].wait_recv()
-
-            @pl.when(c == 12 + h)
-            def _(h=h):
-                copies['xy', h].wait_recv()
-                copies['yx', h].wait_recv()
-                copies['xy core', h].start()
-
-            @pl.when(c == 14 + h)
-            def _(h=h):
-                copies['xy core', h].wait_recv()
+        if 4 <= c < 12:
+            q = (c - 4) // 2
+            if c % 2 == 0:
+                copies['x', q].wait_recv()
+                if q % 2 == 0:
+                    copies['across', q].start()
+                copies['x core', q].start()
+                copies['y', q].wait_recv()
+                if q % 2 == 1:
+                    copies['across', q].start()
+                copies['y core', q].start()
+            else:
+                copies['x core', q].wait_recv()
+                copies['y core', q].wait_recv()
+        if c >= 12:
+            h = (c - 12) // 2
+            if c % 2 == 0:
+                copies['across', 2 * h].wait_recv()
+                copies['across', 2 * h + 1].wait_recv()
+                copies['across core', h].start()
+            else:
+                copies['across core', h].wait_recv()
 
     def mask_value(k):
         return block_mask[me, partner(k)].astype(F32)
@@ -143,23 +158,40 @@
         def _():
             fetch(g + SLOTS).start()
 
-    def masked(y, k, h):
-        cols = pl.ds(pl.multiple_of(h * HALF, HALF), HALF)
-        return (y[k, :, cols].astype(F32) * mask_value(k)).astype(BF16)
+    def forward_pass(copies, y, first, segments):
+        width = y.shape[1]
+        for begin, per_step, steps in segments:
+            def step(i, carry, begin=begin, per_step=per_step, steps=steps):
+                for at in range(steps):
+                    needs = [begin + at * per_step + j for j in range(per_step)]
+                    if any(c == 2 or c >= 4 for c in needs):
+                        @pl.when(i == at)
+                        def _(needs=needs):
+                            for c in needs:
+                                gather_need(copies, c)
+                total = None
+                for j in range(per_step):
+                    c = begin + i * per_step + j
+                    for part in range(2):
+                        k, q = block_quart(c, part)
+                        cols = pl.ds(pl.multiple_of(q * QUART, QUART), QUART)
+                        ymask[:width, (2 * j + part) * QUART:(2 * j + part + 1) * QUART] = (y[k, :, cols].astype(F32) * mask_value(k)).astype(BF16)
+                for j in range(per_step):
+                    fetch(first + begin + i * per_step + j).wait()
+                for j in range(per_step):
+                    g = first + begin + i * per_step + j
+                    term = lax.dot_general(abuf[lax.rem(g, SLOTS)], ymask[:width, j * HALF:(j + 1) * HALF], NT, preferred_element_type=F32)
+                    total = term if total is None else total + term
+                acc[:, :width] += total
+                for j in range(per_step):
+                    next_fetch(first + begin + i * per_step + j)
+                return carry
+            lax.fori_loop(0, steps, step, 0)
 
     copies1 = gather_copies(yall)
     gather_start(copies1)
     acc[...] = jnp.zeros_like(acc)
-
-    def pass1(c, carry):
-        gather_events(copies1, c)
-        k, h = block_half(c)
-        ymask[...] = masked(yall, k, h)
-        fetch(c).wait()
-        acc[...] += lax.dot_general(abuf[lax.rem(c, SLOTS)], ymask[...], NT, preferred_element_type=F32)
-        next_fetch(c)
-        return carry
-    lax.fori_loop(0, CHUNKS, pass1, 0)
+    forward_pass(copies1, yall, 0, ((0, 2, 2), (4, 1, 1), (5, 2, 3), (11, 1, 5)))
 
     hid[...] = jnp.maximum(acc[...], 0.0).astype(BF16)
     y2all[0] = lax.dot_general(wot_bf, hid[...], NT, preferred_element_type=F32).astype(BF16)
@@ -179,16 +211,7 @@
     lax.fori_loop(0, ROWS // 128, turn, 0)
     acc[...] = jnp.zeros_like(acc)
 
-    def pass2(c, carry):
-        gather_events(copies2, c)
-        k, h = block_half(c)
-        ymask[:C_PAD, :] = masked(y2all, k, h)
-        g = c + CHUNKS
-        fetch(g).wait()
-        acc[:, :C_PAD] += lax.dot_general(abuf[lax.rem(g, SLOTS)], ymask[:C_PAD, :], NT, preferred_element_type=F32)
-        next_fetch(g)
-        return carry
-    lax.fori_loop(0, CHUNKS, pass2, 0)
+    forward_pass(copies2, y2all, CHUNKS, ((0, 2, 2), (4, 1, 1), (5, 2, 5), (15, 1, 1)))
 
     def turn2(i, carry):
         at = pl.ds(pl.multiple_of(i * 128, 128), 128)
@@ -237,32 +260,28 @@
 
     def scatter_events(copies, p, r, f, c, pass_on):
         sends = {6: ('xy', 'yx'), 4: ('y raw',), 2: ('x raw',), 0: ()}
-        for q in range(4):
-            for h in range(2):
-                k = 6 - 2 * q
-
-                @pl.when(c == 4 * q + 2 * h)
-                def _(k=k, h=h):
-                    copies['core', k + 1, h].start()
-
-                @pl.when(c == 4 * q + 2 * h + 1)
-                def _(k=k, h=h):
-                    at = pl.ds(h * HALF, HALF)
+        order = [(7, 0), (6, 0), (7, 1), (6, 1)] + [(k, h) for h in range(2) for k in (5, 4, 3, 2)] + [(1, 0), (0, 0), (1, 1), (0, 1)]
+        for at, (k, h) in enumerate(order):
+            @pl.when(c == at)
+            def _(at=at, k=k, h=h):
+                if k % 2 == 1:
+                    copies['core', k, h].start()
+                else:
+                    cols = pl.ds(h * HALF, HALF)
                     copies['core', k + 1, h].wait_recv()
-                    p[k, :, at] = p[k, :, at] + r[k // 2, h]
+                    p[k, :, cols] = p[k, :, cols] + r[k // 2, h]
                     for name in sends[k]:
                         copies[name, h].start()
-
-        for h in range(2):
-            @pl.when(c == pass_on[h])
-            def _(h=h):
-                even, odd = pl.ds(2 * h * QUART, QUART), pl.ds((2 * h + 1) * QUART, QUART)
-                copies['xy', h].wait_recv()
-                p[4, :, even] = p[4, :, even] + f[0, h]
-                copies['y', h].start()
-                copies['yx', h].wait_recv()
-                p[2, :, odd] = p[2, :, odd] + f[1, h]
-                copies['x', h].start()
+                for way, h2 in pass_on.get(at, ()):
+                    if way == 'y':
+                        even = pl.ds(2 * h2 * QUART, QUART)
+                        copies['xy', h2].wait_recv()
+                        p[4, :, even] = p[4, :, even] + f[0, h2]
+                    else:
+                        odd = pl.ds((2 * h2 + 1) * QUART, QUART)
+                        copies['yx', h2].wait_recv()
+                        p[2, :, odd] = p[2, :, odd] + f[1, h2]
+                    copies[way, h2].start()
 
     def scatter_result(copies, p, ix, q):
         h = q // 2
@@ -274,13 +293,13 @@
 
     def pass3(c, carry):
         g = c + 2 * CHUNKS
-        k, h = block_half(g)
-        cols = pl.ds(pl.multiple_of(h * HALF, HALF), HALF)
+        k, q = block_quart(g, 0)
+        cols = pl.ds(pl.multiple_of(q * QUART, HALF), HALF)
         fetch(g).wait()
         part = jnp.dot(lhs1[...], abuf[lax.rem(g, SLOTS)], preferred_element_type=F32)
         pa[k, :, cols] = part * mask_value(k)
         next_fetch(g)
-        scatter_events(copies3, pa, ra, fa, c, (11, 11))
+        scatter_events(copies3, pa, ra, fa, c, {6: (('y', 0),), 7: (('x', 0),), 9: (('y', 1),), 11: (('x', 1),)})
         return carry
     lax.fori_loop(0, CHUNKS, pass3, 0)
     d2t = jnp.concatenate([scatter_result(copies3, pa, ia, q) for q in range(4)], axis=1)
@@ -291,13 +310,13 @@
 
     def pass4(c, carry):
         g = c + 3 * CHUNKS
-        k, h = block_half(g)
-        cols = pl.ds(pl.multiple_of(h * HALF, HALF), HALF)
+        k, q = block_quart(g, 0)
+        cols = pl.ds(pl.multiple_of(q * QUART, HALF), HALF)
         fetch(g).wait()
         part = jnp.dot(lhs2[...], abuf[lax.rem(g, SLOTS)], preferred_element_type=F32)
         pb[k, :, cols] = part * mask_value(k)
         next_fetch(g)
-        scatter_events(copies4, pb, rb, fb, c, (11, 13))
+        scatter_events(copies4, pb, rb, fb, c, {9: (('y', 0),), 10: (('x', 0),), 13: (('y', 1), ('x', 1))})
         return carry
     lax.fori_loop(0, CHUNKS, pass4, 0)
 
@@ -343,7 +362,7 @@
     vmem = pl.BlockSpec(memory_space=pltpu.VMEM)
     hbm = pl.BlockSpec(memory_space=pl.ANY)
     v = pltpu.VMEM
-    copies = 96
+    copies = 112
     loss, gwh, gwo = pl.pallas_call(
         step_kernel,
         out_shape=(jax.ShapeDtypeStruct((1, 1), F32), jax.ShapeDtypeStruct((F_IN, HID), F32), jax.ShapeDtypeStruct((CLASSES, HID), F32)),
@@ -351,13 +370,13 @@
         out_specs=(vmem, vmem, vmem),
         scratch_shapes=[
             v((SLOTS, ROWS, HALF), BF16), v((F_IN, ROWS), BF16), v((ROWS, HID), F32),
-            v((DEVICES, HID, ROWS), BF16), v((DEVICES, C_PAD, ROWS), BF16), v((HID, HALF), BF16), v((ROWS, HID), BF16),
+            v((DEVICES, HID, ROWS), BF16), v((DEVICES, C_PAD, ROWS), BF16), v((HID, ROWS), BF16), v((ROWS, HID), BF16),
             v((HID, ROWS), F32), v((C_PAD, ROWS), F32), v((128, 128), F32), v((C_PAD, ROWS), BF16), v((HID, ROWS), BF16),
             v((DEVICES, 8, 128), F32),
             v((DEVICES, C_PAD, ROWS), F32), v((4, 2, C_PAD, HALF), F32), v((2, 2, C_PAD, QUART), F32), v((2, 4, C_PAD, QUART), F32),
             v((DEVICES, HID, ROWS), F32), v((4, 2, HID, HALF), F32), v((2, 2, HID, QUART), F32), v((2, 4, HID, QUART), F32),
             v((SUM_ROWS, HID), F32), v((SUM_ROWS // 2, HID), F32), v((2, 2, SUM_ROWS // 4, HID), F32), v((SUM_ROWS // 2, HID), F32),
-            pltpu.SemaphoreType.DMA((SLOTS,)), pltpu.SemaphoreType.DMA((1,)),
+            pltpu.SemaphoreType.DMA((SLOTS, 2)), pltpu.SemaphoreType.DMA((1,)),
             pltpu.SemaphoreType.DMA((copies,)), pltpu.SemaphoreType.DMA((copies,)),
         ],
         compiler_params=pltpu.CompilerParams(collective_id=0, has_side_effects=True, vmem_limit_bytes=67043328),

time: 145 us -> 132 us (0.910)
  Pallas kernels: 139 us -> 126 us
    pallas_call x1, Pallas kernels: 139 us -> 126 us  [device_step(): pl.pallas_call(step_kernel, out_shape=(jax.ShapeDtypeStruct((1, 1), F32),...]
where the time goes in v3:
time: 132 us
  Pallas kernels  126 us (95%)
  local copies, waits for them, and re-layouts  3.05 us (2%)
  between operations  2.39 us (2%)
    pallas_call x1, Pallas kernels, device_step(): pl.pallas_call(step_kernel, out_shape=(jax.ShapeDtypeStruct((1, 1), F32),...  126 us
    unnamed x2, local copies, waits for them, and re-layouts  3.05 us

profile of v3, /device:TPU:0, one launch (start us, length us, event | category | flops | bytes accessed | tf_op | source)
XLA Modules:
  0.0 131.7 jit_solution(12323490755713362073)
XLA Ops:
  0.6 126.3 %gcn_step.1 = (f32[1,1]{1,0:T(1,128)}, f32[602,128]{1,0:T(8,128)}, f32[41,128]{1,0:T(8,128)}) custom-call(bf16[2048,16384]{1,0:T(8,128)(2,1)} %adj.1, bf16[602,2048]{1,0:T(8,128)(2,1)} %bitcast.6, f32[602,128]{1,0:T(8,128)} %wh.1, f32[41,128]{1,0:T(8,128)} %bitcast.7, s32[1,2048]{1,0:T(1,128)} %bitcast.9, s32[1,2048]{1,0:T(1,128)} %bitcast.10, s32[8,8]{1,0:T(8,128)} %block_mask.1), custom_call_target="tpu_custom_call" | custom-call | tf_op jit(solution)/shard_map/gcn_step/pallas_call | solution.py:366
  127.5 1.7 %copy.14 = f32[602,128]{1,0:T(8,128)} copy(f32[602,128]{1,0:T(8,128)} %get-tuple-element.13) | data formatting | bytes 616448
  129.2 1.3 %copy.15 = f32[128,41]{0,1:T(8,128)} copy(f32[128,41]{0,1:T(8,128)} %bitcast.8) | data formatting | bytes 41984

commit v4 on v3

--- a/solution.py
+++ b/solution.py
@@ -17,7 +17,7 @@
 C_PAD = 48
 HALF = ROWS // 2
 QUART = ROWS // 4
-SLOTS = 6
+SLOTS = 8
 CHUNKS = NODES // HALF
 SUM_ROWS = 672
 GWO_ROW = 608
@@ -25,9 +25,9 @@
 NT = (((1,), (1,)), ((), ()))
 
 
-def step_kernel(adj, feat, wh, wo, labels, mask, block_mask, loss_out, gwh_out, gwo_out,
-                abuf, xbuf, acc, yall, y2all, ymask, hid, z1t, z2t, wpad, lhs1, lhs2, cnt,
-                pa, ra, fa, ia, pb, rb, fb, ib, gpart, gpair, gacross, gback,
+def step_kernel(adj, feat, wh_in, wo_in, labels_in, mask_in, block_mask, sums_out,
+                abuf, xbuf, wh, wo, labels, mask, acc, yall, y2all, ymask, hid, z1t, wpad, lhs1, lhs2, cnt,
+                ra, fa, ia, pb, rb, fb, ib, gpart, gpair, gacross,
                 asem, xsem, ssem, rsem):
     me = lax.axis_index(AXIS_NAME)
     bits = (lax.rem(me, 2), lax.rem(me // 2, 2), me // 4)
@@ -78,11 +78,17 @@
 
     xcopy = pltpu.make_async_copy(feat, xbuf, xsem.at[0])
     xcopy.start()
+    small = [pltpu.make_async_copy(src, dst, xsem.at[1 + i]) for i, (src, dst) in
+             enumerate(((wh_in, wh), (wo_in, wo), (labels_in, labels), (mask_in, mask)))]
+    for copy in small:
+        copy.start()
     fetch(jnp.int32(0)).start()
     barrier = pltpu.get_barrier_semaphore()
     for k in range(1, DEVICES):
         pl.semaphore_signal(barrier, inc=1, device_id=(peers[k],), device_id_type=MESH)
 
+    for copy in small:
+        copy.wait()
     wpad[...] = jnp.zeros_like(wpad)
     wpad[:CLASSES, :] = wo[...]
     wot_bf = wpad[:C_PAD, :].astype(BF16)
@@ -91,7 +97,7 @@
     weight = mask[...].astype(F32)
     cnt[0] = jnp.broadcast_to(jnp.sum(weight, axis=1, keepdims=True), (8, 128))
     xcopy.wait()
-    for g in range(1, SLOTS):
+    for g in range(1, SLOTS - 2):
         fetch(jnp.int32(g)).start()
     yall[0] = jnp.dot(wh_t, xbuf[...], preferred_element_type=F32).astype(BF16)
     pl.semaphore_wait(barrier, DEVICES - 1)
@@ -153,11 +159,6 @@
     def mask_value(k):
         return block_mask[me, partner(k)].astype(F32)
 
-    def next_fetch(g):
-        @pl.when(g + SLOTS < 4 * CHUNKS)
-        def _():
-            fetch(g + SLOTS).start()
-
     def forward_pass(copies, y, first, segments):
         width = y.shape[1]
         for begin, per_step, steps in segments:
@@ -179,12 +180,12 @@
                 for j in range(per_step):
                     fetch(first + begin + i * per_step + j).wait()
                 for j in range(per_step):
+                    fetch(first + begin + i * per_step + j + SLOTS - 2).start()
+                for j in range(per_step):
                     g = first + begin + i * per_step + j
                     term = lax.dot_general(abuf[lax.rem(g, SLOTS)], ymask[:width, j * HALF:(j + 1) * HALF], NT, preferred_element_type=F32)
                     total = term if total is None else total + term
                 acc[:, :width] += total
-                for j in range(per_step):
-                    next_fetch(first + begin + i * per_step + j)
                 return carry
             lax.fori_loop(0, steps, step, 0)
 
@@ -206,7 +207,7 @@
 
     def turn(i, carry):
         at = pl.ds(pl.multiple_of(i * 128, 128), 128)
-        z1t[:, at] = acc[at, :].T
+        z1t[:, at] = (acc[at, :] > 0.0).astype(F32).T.astype(BF16)
         return carry
     lax.fori_loop(0, ROWS // 128, turn, 0)
     acc[...] = jnp.zeros_like(acc)
@@ -215,7 +216,7 @@
 
     def turn2(i, carry):
         at = pl.ds(pl.multiple_of(i * 128, 128), 128)
-        z2t[:, at] = acc[at, :].T[:C_PAD]
+        pb[0, :C_PAD, at] = acc[at, :].T[:C_PAD]
         return carry
     lax.fori_loop(0, ROWS // 128, turn2, 0)
     for copy in count_copies:
@@ -226,7 +227,7 @@
     loss = jnp.zeros((1, 1), F32)
     for q in range(4):
         at = pl.ds(q * QUART, QUART)
-        z = z2t[:, at]
+        z = pb[0, :C_PAD, at]
         row = lax.broadcasted_iota(jnp.int32, (C_PAD, QUART), 0)
         z = jnp.where(row < CLASSES, z, -jnp.inf)
         top = jnp.max(z, axis=0, keepdims=True)
@@ -289,6 +290,7 @@
             copies[name, h].wait_recv()
         return (p[0, :, pl.ds(q * QUART, QUART)] + ix[0, q] + ix[1, q]).astype(BF16)
 
+    pa = pb.at[:, pl.ds(0, C_PAD), :]
     copies3 = scatter_copies(pa, ra, fa, ia)
 
     def pass3(c, carry):
@@ -296,15 +298,18 @@
         k, q = block_quart(g, 0)
         cols = pl.ds(pl.multiple_of(q * QUART, HALF), HALF)
         fetch(g).wait()
+        fetch(g + SLOTS - 2).start()
         part = jnp.dot(lhs1[...], abuf[lax.rem(g, SLOTS)], preferred_element_type=F32)
         pa[k, :, cols] = part * mask_value(k)
-        next_fetch(g)
         scatter_events(copies3, pa, ra, fa, c, {6: (('y', 0),), 7: (('x', 0),), 9: (('y', 1),), 11: (('x', 1),)})
         return carry
     lax.fori_loop(0, CHUNKS, pass3, 0)
     d2t = jnp.concatenate([scatter_result(copies3, pa, ia, q) for q in range(4)], axis=1)
     back = jnp.dot(wo_bf, d2t, preferred_element_type=F32)
-    lhs2[...] = jnp.where(z1t[...] > 0.0, back, 0.0).astype(BF16)
+    lhs2[...] = jnp.where(z1t[...].astype(F32) > 0.0, back, 0.0).astype(BF16)
+
+    for copy in copies3.values():
+        copy.wait_send()
 
     copies4 = scatter_copies(pb, rb, fb, ib)
 
@@ -313,9 +318,12 @@
         k, q = block_quart(g, 0)
         cols = pl.ds(pl.multiple_of(q * QUART, HALF), HALF)
         fetch(g).wait()
+
+        @pl.when(g + SLOTS - 2 < 4 * CHUNKS)
+        def _():
+            fetch(g + SLOTS - 2).start()
         part = jnp.dot(lhs2[...], abuf[lax.rem(g, SLOTS)], preferred_element_type=F32)
         pb[k, :, cols] = part * mask_value(k)
-        next_fetch(g)
         scatter_events(copies4, pb, rb, fb, c, {9: (('y', 0),), 10: (('x', 0),), 13: (('y', 1), ('x', 1))})
         return carry
     lax.fori_loop(0, CHUNKS, pass4, 0)
@@ -323,7 +331,7 @@
     gpart[F_IN // 8 * 8:GWO_ROW, :] = jnp.zeros((8, HID), F32)
     gpart[GWO_ROW:LOSS_ROW, :] = jnp.dot(d2t, hid[...], preferred_element_type=F32)
     gpart[LOSS_ROW:SUM_ROWS, :] = jnp.broadcast_to(loss / label_count, (SUM_ROWS - LOSS_ROW, HID))
-    for copy in list(copies2.values()) + count_copies + list(copies3.values()):
+    for copy in list(copies2.values()) + count_copies:
         copy.wait_send()
     for q in range(4):
         term = lax.dot_general(xbuf[:, q * QUART:(q + 1) * QUART], scatter_result(copies4, pb, ib, q), NT, preferred_element_type=F32)
@@ -347,15 +355,20 @@
         for q in range(2):
             copies[q].wait()
             gpart[quarts[q], :] = gpart[quarts[q], :] + gacross[step, q]
-    final = remote(gpart.at[mine, :], gback, 1)
+    final = remote(gpart.at[mine, :], sums_out.at[mine, :], 1)
     final.start()
+    keep = pltpu.make_async_copy(gpart.at[mine, :], sums_out.at[mine, :], xsem.at[0])
+    keep.start()
     for copy in copies4.values():
         copy.wait_send()
+    keep.wait()
     final.wait()
-    gpart[other, :] = gback[...]
-    gwh_out[...] = gpart[:F_IN, :]
-    gwo_out[...] = gpart[GWO_ROW:GWO_ROW + CLASSES, :]
-    loss_out[...] = gpart[LOSS_ROW:LOSS_ROW + 1, 0:1]
+
+
+def cut_kernel(sums, loss_out, gwh_out, gwo_out):
+    gwh_out[...] = sums[:F_IN, :]
+    gwo_out[...] = sums[GWO_ROW:GWO_ROW + CLASSES, :]
+    loss_out[...] = sums[LOSS_ROW:LOSS_ROW + 1, 0:1]
 
 
 def device_step(adj, feat, w_hidden, w_output, labels, train_mask, block_mask):
@@ -363,25 +376,33 @@
     hbm = pl.BlockSpec(memory_space=pl.ANY)
     v = pltpu.VMEM
     copies = 112
-    loss, gwh, gwo = pl.pallas_call(
+    sums = pl.pallas_call(
         step_kernel,
-        out_shape=(jax.ShapeDtypeStruct((1, 1), F32), jax.ShapeDtypeStruct((F_IN, HID), F32), jax.ShapeDtypeStruct((CLASSES, HID), F32)),
-        in_specs=[hbm, hbm, vmem, vmem, vmem, vmem, pl.BlockSpec(memory_space=pltpu.SMEM)],
-        out_specs=(vmem, vmem, vmem),
+        out_shape=jax.ShapeDtypeStruct((SUM_ROWS, HID), F32),
+        in_specs=[hbm] * 6 + [pl.BlockSpec(memory_space=pltpu.SMEM)],
+        out_specs=hbm,
         scratch_shapes=[
-            v((SLOTS, ROWS, HALF), BF16), v((F_IN, ROWS), BF16), v((ROWS, HID), F32),
+            v((SLOTS, ROWS, HALF), BF16), v((F_IN, ROWS), BF16), v((F_IN, HID), F32), v((CLASSES, HID), F32), v((1, ROWS), jnp.int32), v((1, ROWS), jnp.int32), v((ROWS, HID), F32),
             v((DEVICES, HID, ROWS), BF16), v((DEVICES, C_PAD, ROWS), BF16), v((HID, ROWS), BF16), v((ROWS, HID), BF16),
-            v((HID, ROWS), F32), v((C_PAD, ROWS), F32), v((128, 128), F32), v((C_PAD, ROWS), BF16), v((HID, ROWS), BF16),
+            v((HID, ROWS), BF16), v((128, 128), F32), v((C_PAD, ROWS), BF16), v((HID, ROWS), BF16),
             v((DEVICES, 8, 128), F32),
-            v((DEVICES, C_PAD, ROWS), F32), v((4, 2, C_PAD, HALF), F32), v((2, 2, C_PAD, QUART), F32), v((2, 4, C_PAD, QUART), F32),
+            v((4, 2, C_PAD, HALF), F32), v((2, 2, C_PAD, QUART), F32), v((2, 4, C_PAD, QUART), F32),
             v((DEVICES, HID, ROWS), F32), v((4, 2, HID, HALF), F32), v((2, 2, HID, QUART), F32), v((2, 4, HID, QUART), F32),
-            v((SUM_ROWS, HID), F32), v((SUM_ROWS // 2, HID), F32), v((2, 2, SUM_ROWS // 4, HID), F32), v((SUM_ROWS // 2, HID), F32),
-            pltpu.SemaphoreType.DMA((SLOTS, 2)), pltpu.SemaphoreType.DMA((1,)),
+            v((SUM_ROWS, HID), F32), v((SUM_ROWS // 2, HID), F32), v((2, 2, SUM_ROWS // 4, HID), F32),
+            pltpu.SemaphoreType.DMA((SLOTS, 2)), pltpu.SemaphoreType.DMA((5,)),
             pltpu.SemaphoreType.DMA((copies,)), pltpu.SemaphoreType.DMA((copies,)),
         ],
         compiler_params=pltpu.CompilerParams(collective_id=0, has_side_effects=True, vmem_limit_bytes=67043328),
         name='gcn_step',
     )(adj, feat.T, w_hidden, w_output.T, labels.reshape(1, ROWS), train_mask.reshape(1, ROWS), block_mask)
+    loss, gwh, gwo = pl.pallas_call(
+        cut_kernel,
+        out_shape=(jax.ShapeDtypeStruct((1, 1), F32), jax.ShapeDtypeStruct((F_IN, HID), F32), jax.ShapeDtypeStruct((CLASSES, HID), F32)),
+        in_specs=[vmem],
+        out_specs=(vmem, vmem, vmem),
+        compiler_params=pltpu.CompilerParams(vmem_limit_bytes=4 * 2**20),
+        name='cut',
+    )(sums)
     return loss[0, 0], gwh, gwo.T
 
 

time: 132 us -> 127 us (0.962)
  local copies, waits for them, and re-layouts: 3.05 us -> 0.97 us
  between operations: 2.39 us -> 0.65 us
    unnamed x2, local copies, waits for them, and re-layouts: 3.05 us -> 0.97 us
    pallas_call x1 -> x2, Pallas kernels: 126 us -> 126 us  [the longest x1 125 us: device_step(): pl.pallas_call(step_kernel, out_shape=jax.ShapeDtypeStruct((SUM_ROWS, HID...]
where the time goes in v4:
time: 127 us
  Pallas kernels  126 us (99%)
    pallas_call x1, Pallas kernels, device_step(): pl.pallas_call(step_kernel, out_shape=jax.ShapeDtypeStruct((SUM_ROWS, HID...  125 us

profile of v4, /device:TPU:0, one launch (start us, length us, event | category | flops | bytes accessed | tf_op | source)
XLA Modules:
  0.0 127.2 jit_solution(16732424690574302360)
XLA Ops:
  0.6 124.8 %gcn_step.1.sums = f32[672,128]{1,0:T(8,128)} custom-call(bf16[2048,16384]{1,0:T(8,128)(2,1)} %adj.1, bf16[602,2048]{1,0:T(8,128)(2,1)} %bitcast.6, f32[602,128]{1,0:T(8,128)} %wh_in.1, f32[41,128]{1,0:T(8,128)} %bitcast.7, s32[1,2048]{1,0:T(1,128)} %bitcast.8, s32[1,2048]{1,0:T(1,128)} %bitcast.9, s32[8,8]{1,0:T(8,128)} %block_mask.1), custom_call_target="tpu_custom_call" | custom-call | tf_op jit(solution)/shard_map/gcn_step/pallas_call | solution.py:379
  125.4 0.0 copy-start
  125.5 1.0 copy-done
  126.4 0.7 cut.1
Async XLA Ops:
  125.4 1.0 copy-start

commit v5 on v4

--- a/solution.py
+++ b/solution.py
@@ -26,7 +26,7 @@
 
 
 def step_kernel(adj, feat, wh_in, wo_in, labels_in, mask_in, block_mask, sums_out,
-                abuf, xbuf, wh, wo, labels, mask, acc, yall, y2all, ymask, hid, z1t, wpad, lhs1, lhs2, cnt,
+                abuf, xbuf, wh, wo, labels, mask, acc, yall, y2all, ymask, hid, hidt, wpad, lhs, cnt,
                 ra, fa, ia, pb, rb, fb, ib, gpart, gpair, gacross,
                 asem, xsem, ssem, rsem):
     me = lax.axis_index(AXIS_NAME)
@@ -68,12 +68,8 @@
 
     fetch = Fetch
 
-    used = [0]
-
-    def remote(src, dst, k):
-        i = used[0]
-        used[0] += 1
-        return pltpu.make_async_remote_copy(src_ref=src, dst_ref=dst, send_sem=ssem.at[i], recv_sem=rsem.at[i],
+    def remote(src, dst, k, send, recv):
+        return pltpu.make_async_remote_copy(src_ref=src, dst_ref=dst, send_sem=ssem.at[send], recv_sem=rsem.at[recv],
                                             device_id=(peers[k],), device_id_type=MESH)
 
     xcopy = pltpu.make_async_copy(feat, xbuf, xsem.at[0])
@@ -83,6 +79,7 @@
     for copy in small:
         copy.start()
     fetch(jnp.int32(0)).start()
+    fetch(jnp.int32(1)).start()
     barrier = pltpu.get_barrier_semaphore()
     for k in range(1, DEVICES):
         pl.semaphore_signal(barrier, inc=1, device_id=(peers[k],), device_id_type=MESH)
@@ -97,30 +94,34 @@
     weight = mask[...].astype(F32)
     cnt[0] = jnp.broadcast_to(jnp.sum(weight, axis=1, keepdims=True), (8, 128))
     xcopy.wait()
-    for g in range(1, SLOTS - 2):
+    for g in range(2, SLOTS - 2):
         fetch(jnp.int32(g)).start()
     yall[0] = jnp.dot(wh_t, xbuf[...], preferred_element_type=F32).astype(BF16)
     pl.semaphore_wait(barrier, DEVICES - 1)
 
-    def gather_copies(y):
+    def gather_copies(y, send, recv):
         def half(k, h):
             return y.at[k, :, pl.ds(h * HALF, HALF)]
 
         def quart(k, q):
             return y.at[k, :, pl.ds(q * QUART, QUART)]
 
-        copies = {'own': remote(y.at[0], y.at[1], 1)}
+        copies = {'own': remote(y.at[0], y.at[1], 1, send, recv)}
         for q in range(4):
-            copies['x', q] = remote(quart(0, q), quart(2, q), 2)
-            copies['y', q] = remote(quart(0, q), quart(4, q), 4)
-            copies['x core', q] = remote(quart(2, q), quart(3, q), 1)
-            copies['y core', q] = remote(quart(4, q), quart(5, q), 1)
+            copies['x', q] = remote(quart(0, q), quart(2, q), 2, send, recv + 1 + q)
+            copies['y', q] = remote(quart(0, q), quart(4, q), 4, send, recv + 1 + q)
+            copies['x core', q] = remote(quart(2, q), quart(3, q), 1, send, recv + 5 + q)
+            copies['y core', q] = remote(quart(4, q), quart(5, q), 1, send, recv + 5 + q)
+            copies['both', q] = remote(half(0, 0), half(0, 0), 2, send, recv + 1 + q)
+            copies['both core', q] = remote(half(0, 0), half(0, 0), 1, send, recv + 5 + q)
             if q % 2 == 0:
-                copies['across', q] = remote(quart(2, q), quart(6, q), 4)
+                copies['across', q] = remote(quart(2, q), quart(6, q), 4, send, recv + 9 + q // 2)
             else:
-                copies['across', q] = remote(quart(4, q), quart(6, q), 2)
+                copies['across', q] = remote(quart(4, q), quart(6, q), 2, send, recv + 9 + q // 2)
         for h in range(2):
-            copies['across core', h] = remote(half(6, h), half(7, h), 1)
+            copies['across both', h] = remote(half(0, 0), half(0, 0), 2, send, recv + 9 + h)
+            copies['across core', h] = remote(half(6, h), half(7, h), 1, send, recv + 11 + h)
+        copies['sent'] = remote(y.at[pl.ds(0, 7)], y.at[pl.ds(0, 7)], 1, send, recv)
         return copies
 
     def gather_start(copies):
@@ -136,22 +137,16 @@
         if 4 <= c < 12:
             q = (c - 4) // 2
             if c % 2 == 0:
-                copies['x', q].wait_recv()
-                if q % 2 == 0:
-                    copies['across', q].start()
+                copies['both', q].wait_recv()
+                copies['across', q].start()
                 copies['x core', q].start()
-                copies['y', q].wait_recv()
-                if q % 2 == 1:
-                    copies['across', q].start()
                 copies['y core', q].start()
             else:
-                copies['x core', q].wait_recv()
-                copies['y core', q].wait_recv()
+                copies['both core', q].wait_recv()
         if c >= 12:
             h = (c - 12) // 2
             if c % 2 == 0:
-                copies['across', 2 * h].wait_recv()
-                copies['across', 2 * h + 1].wait_recv()
+                copies['across both', h].wait_recv()
                 copies['across core', h].start()
             else:
                 copies['across core', h].wait_recv()
@@ -189,7 +184,7 @@
                 return carry
             lax.fori_loop(0, steps, step, 0)
 
-    copies1 = gather_copies(yall)
+    copies1 = gather_copies(yall, 0, 0)
     gather_start(copies1)
     acc[...] = jnp.zeros_like(acc)
     forward_pass(copies1, yall, 0, ((0, 2, 2), (4, 1, 1), (5, 2, 3), (11, 1, 5)))
@@ -197,34 +192,28 @@
     hid[...] = jnp.maximum(acc[...], 0.0).astype(BF16)
     y2all[0] = lax.dot_general(wot_bf, hid[...], NT, preferred_element_type=F32).astype(BF16)
 
-    copies2 = gather_copies(y2all)
+    copies2 = gather_copies(y2all, 1, 13)
     gather_start(copies2)
-    count_copies = [remote(cnt.at[0], cnt.at[k], k) for k in range(1, DEVICES)]
+    count_copies = [remote(cnt.at[0], cnt.at[k], k, 2, 26) for k in range(1, DEVICES)]
+    counts = remote(cnt.at[pl.ds(1, 7)], cnt.at[pl.ds(1, 7)], 1, 2, 26)
     for copy in count_copies:
         copy.start()
-    for copy in copies1.values():
-        copy.wait_send()
-
-    def turn(i, carry):
-        at = pl.ds(pl.multiple_of(i * 128, 128), 128)
-        z1t[:, at] = (acc[at, :] > 0.0).astype(F32).T.astype(BF16)
-        return carry
-    lax.fori_loop(0, ROWS // 128, turn, 0)
+    copies1['sent'].wait_send()
+    ident = (lax.broadcasted_iota(jnp.int32, (HID, HID), 0) == lax.broadcasted_iota(jnp.int32, (HID, HID), 1)).astype(BF16)
+    hidt[...] = lax.dot_general(ident, hid[...], NT, preferred_element_type=F32).astype(BF16)
     acc[...] = jnp.zeros_like(acc)
 
     forward_pass(copies2, y2all, CHUNKS, ((0, 2, 2), (4, 1, 1), (5, 2, 5), (15, 1, 1)))
 
-    def turn2(i, carry):
-        at = pl.ds(pl.multiple_of(i * 128, 128), 128)
+    for i in range(ROWS // 128):
+        at = pl.ds(i * 128, 128)
         pb[0, :C_PAD, at] = acc[at, :].T[:C_PAD]
-        return carry
-    lax.fori_loop(0, ROWS // 128, turn2, 0)
-    for copy in count_copies:
-        copy.wait_recv()
+    counts.wait_recv()
     label_count = cnt[0, 0:1, 0:1]
     for k in range(1, DEVICES):
         label_count = label_count + cnt[k, 0:1, 0:1]
     loss = jnp.zeros((1, 1), F32)
+    lhs[C_PAD:, :] = jnp.zeros((HID - C_PAD, ROWS), BF16)
     for q in range(4):
         at = pl.ds(q * QUART, QUART)
         z = pb[0, :C_PAD, at]
@@ -237,26 +226,28 @@
         w = mask[:, at].astype(F32)
         loss = loss + jnp.sum(w * (log_norm - picked), axis=1, keepdims=True)
         prob = jnp.exp(z - log_norm)
-        lhs1[:, at] = ((prob - hot.astype(F32)) * (w / label_count)).astype(BF16)
-
-    def scatter_copies(p, r, f, ix):
+        lhs[:C_PAD, at] = ((prob - hot.astype(F32)) * (w / label_count)).astype(BF16)
+
+    def scatter_copies(p, r, f, ix, send, recv):
         def half(k, h):
             return p.at[k, :, pl.ds(h * HALF, HALF)]
 
         def quart(k, q):
             return p.at[k, :, pl.ds(q * QUART, QUART)]
 
-        copies = {}
+        copies = {'sent': remote(p.at[pl.ds(0, 7)], p.at[pl.ds(0, 7)], 1, send, recv)}
         for h in range(2):
             even, odd = 2 * h, 2 * h + 1
             for k in (7, 5, 3, 1):
-                copies['core', k, h] = remote(half(k, h), r.at[k // 2, h], 1)
-            copies['xy', h] = remote(quart(6, even), f.at[0, h], 2)
-            copies['yx', h] = remote(quart(6, odd), f.at[1, h], 4)
-            copies['y raw', h] = remote(quart(4, odd), ix.at[1, odd], 4)
-            copies['x raw', h] = remote(quart(2, even), ix.at[0, even], 2)
-            copies['y', h] = remote(quart(4, even), ix.at[1, even], 4)
-            copies['x', h] = remote(quart(2, odd), ix.at[0, odd], 2)
+                copies['core', k, h] = remote(half(k, h), r.at[k // 2, h], 1, send, recv + k - 1 + h)
+            copies['xy', h] = remote(quart(6, even), f.at[0, h], 2, send, recv + 8 + h)
+            copies['yx', h] = remote(quart(6, odd), f.at[1, h], 4, send, recv + 10 + h)
+            copies['y raw', h] = remote(quart(4, odd), ix.at[1, odd], 4, send, recv + 12 + odd)
+            copies['x raw', h] = remote(quart(2, even), ix.at[0, even], 2, send, recv + 12 + even)
+            copies['y', h] = remote(quart(4, even), ix.at[1, even], 4, send, recv + 12 + even)
+            copies['x', h] = remote(quart(2, odd), ix.at[0, odd], 2, send, recv + 12 + odd)
+            copies['both', even] = remote(half(0, 0), half(0, 0), 2, send, recv + 12 + even)
+            copies['both', odd] = remote(half(0, 0), half(0, 0), 2, send, recv + 12 + odd)
         return copies
 
     def scatter_events(copies, p, r, f, c, pass_on):
@@ -285,13 +276,11 @@
                     copies[way, h2].start()
 
     def scatter_result(copies, p, ix, q):
-        h = q // 2
-        for name in (('y', 'x raw') if q % 2 == 0 else ('y raw', 'x')):
-            copies[name, h].wait_recv()
+        copies['both', q].wait_recv()
         return (p[0, :, pl.ds(q * QUART, QUART)] + ix[0, q] + ix[1, q]).astype(BF16)
 
     pa = pb.at[:, pl.ds(0, C_PAD), :]
-    copies3 = scatter_copies(pa, ra, fa, ia)
+    copies3 = scatter_copies(pa, ra, fa, ia, 3, 27)
 
     def pass3(c, carry):
         g = c + 2 * CHUNKS
@@ -299,19 +288,18 @@
         cols = pl.ds(pl.multiple_of(q * QUART, HALF), HALF)
         fetch(g).wait()
         fetch(g + SLOTS - 2).start()
-        part = jnp.dot(lhs1[...], abuf[lax.rem(g, SLOTS)], preferred_element_type=F32)
-        pa[k, :, cols] = part * mask_value(k)
+        part = jnp.dot(lhs[...], abuf[lax.rem(g, SLOTS)], preferred_element_type=F32)
+        pa[k, :, cols] = part[:C_PAD] * mask_value(k)
         scatter_events(copies3, pa, ra, fa, c, {6: (('y', 0),), 7: (('x', 0),), 9: (('y', 1),), 11: (('x', 1),)})
         return carry
     lax.fori_loop(0, CHUNKS, pass3, 0)
     d2t = jnp.concatenate([scatter_result(copies3, pa, ia, q) for q in range(4)], axis=1)
     back = jnp.dot(wo_bf, d2t, preferred_element_type=F32)
-    lhs2[...] = jnp.where(z1t[...].astype(F32) > 0.0, back, 0.0).astype(BF16)
-
-    for copy in copies3.values():
-        copy.wait_send()
-
-    copies4 = scatter_copies(pb, rb, fb, ib)
+    lhs[...] = jnp.where(hidt[...].astype(F32) > 0.0, back, 0.0).astype(BF16)
+
+    copies3['sent'].wait_send()
+
+    copies4 = scatter_copies(pb, rb, fb, ib, 4, 43)
 
     def pass4(c, carry):
         g = c + 3 * CHUNKS
@@ -322,7 +310,7 @@
         @pl.when(g + SLOTS - 2 < 4 * CHUNKS)
         def _():
             fetch(g + SLOTS - 2).start()
-        part = jnp.dot(lhs2[...], abuf[lax.rem(g, SLOTS)], preferred_element_type=F32)
+        part = jnp.dot(lhs[...], abuf[lax.rem(g, SLOTS)], preferred_element_type=F32)
         pb[k, :, cols] = part * mask_value(k)
         scatter_events(copies4, pb, rb, fb, c, {9: (('y', 0),), 10: (('x', 0),), 13: (('y', 1), ('x', 1))})
         return carry
@@ -331,8 +319,8 @@
     gpart[F_IN // 8 * 8:GWO_ROW, :] = jnp.zeros((8, HID), F32)
     gpart[GWO_ROW:LOSS_ROW, :] = jnp.dot(d2t, hid[...], preferred_element_type=F32)
     gpart[LOSS_ROW:SUM_ROWS, :] = jnp.broadcast_to(loss / label_count, (SUM_ROWS - LOSS_ROW, HID))
-    for copy in list(copies2.values()) + count_copies:
-        copy.wait_send()
+    copies2['sent'].wait_send()
+    counts.wait_send()
     for q in range(4):
         term = lax.dot_general(xbuf[:, q * QUART:(q + 1) * QUART], scatter_result(copies4, pb, ib, q), NT, preferred_element_type=F32)
         if q == 0:
@@ -343,24 +331,31 @@
     half_rows, quart_rows = SUM_ROWS // 2, SUM_ROWS // 4
     mine = pl.ds(pl.multiple_of(bits[0] * half_rows, 8), half_rows)
     other = pl.ds(pl.multiple_of((1 - bits[0]) * half_rows, 8), half_rows)
-    swap = remote(gpart.at[other, :], gpair, 1)
+    swap = remote(gpart.at[other, :], gpair, 1, 5, 59)
     swap.start()
     swap.wait()
     gpart[mine, :] = gpart[mine, :] + gpair[...]
-    quarts = [pl.ds(pl.multiple_of(bits[0] * half_rows + q * quart_rows, 8), quart_rows) for q in range(2)]
-    for step, ways in enumerate(((2, 4), (4, 2))):
-        copies = [remote(gpart.at[quarts[q], :], gacross.at[step, q], ways[q]) for q in range(2)]
-        for copy in copies:
-            copy.start()
-        for q in range(2):
-            copies[q].wait()
-            gpart[quarts[q], :] = gpart[quarts[q], :] + gacross[step, q]
-    final = remote(gpart.at[mine, :], sums_out.at[mine, :], 1)
+    first = [{}, {}]
+    pieces = [(q, begin, size) for begin, size in ((0, 88), (88, quart_rows - 88)) for q in range(2)]
+    rows = []
+    for n, (q, begin, size) in enumerate(pieces):
+        at = pl.ds(pl.multiple_of(bits[0] * half_rows + q * quart_rows + begin, 8), size)
+        rows.append(at)
+        for step in range(2):
+            way = (2, 4)[(q + step) % 2]
+            first[step][n] = remote(gpart.at[at, :], gacross.at[step, q, pl.ds(begin, size), :], way, 6 + 4 * step + n, 60 + 4 * step + n)
+        first[0][n].start()
+    for step in range(2):
+        for n, (q, begin, size) in enumerate(pieces):
+            first[step][n].wait()
+            gpart[rows[n], :] = gpart[rows[n], :] + gacross[step, q, begin:begin + size, :]
+            if step == 0:
+                first[1][n].start()
+    final = remote(gpart.at[mine, :], sums_out.at[mine, :], 1, 14, 68)
     final.start()
     keep = pltpu.make_async_copy(gpart.at[mine, :], sums_out.at[mine, :], xsem.at[0])
     keep.start()
-    for copy in copies4.values():
-        copy.wait_send()
+    copies4['sent'].wait_send()
     keep.wait()
     final.wait()
 
@@ -375,7 +370,7 @@
     vmem = pl.BlockSpec(memory_space=pltpu.VMEM)
     hbm = pl.BlockSpec(memory_space=pl.ANY)
     v = pltpu.VMEM
-    copies = 112
+    sends, arrivals = 15, 69
     sums = pl.pallas_call(
         step_kernel,
         out_shape=jax.ShapeDtypeStruct((SUM_ROWS, HID), F32),
@@ -384,13 +379,13 @@
         scratch_shapes=[
             v((SLOTS, ROWS, HALF), BF16), v((F_IN, ROWS), BF16), v((F_IN, HID), F32), v((CLASSES, HID), F32), v((1, ROWS), jnp.int32), v((1, ROWS), jnp.int32), v((ROWS, HID), F32),
             v((DEVICES, HID, ROWS), BF16), v((DEVICES, C_PAD, ROWS), BF16), v((HID, ROWS), BF16), v((ROWS, HID), BF16),
-            v((HID, ROWS), BF16), v((128, 128), F32), v((C_PAD, ROWS), BF16), v((HID, ROWS), BF16),
+            v((HID, ROWS), BF16), v((128, 128), F32), v((HID, ROWS), BF16),
             v((DEVICES, 8, 128), F32),
             v((4, 2, C_PAD, HALF), F32), v((2, 2, C_PAD, QUART), F32), v((2, 4, C_PAD, QUART), F32),
             v((DEVICES, HID, ROWS), F32), v((4, 2, HID, HALF), F32), v((2, 2, HID, QUART), F32), v((2, 4, HID, QUART), F32),
             v((SUM_ROWS, HID), F32), v((SUM_ROWS // 2, HID), F32), v((2, 2, SUM_ROWS // 4, HID), F32),
             pltpu.SemaphoreType.DMA((SLOTS, 2)), pltpu.SemaphoreType.DMA((5,)),
-            pltpu.SemaphoreType.DMA((copies,)), pltpu.SemaphoreType.DMA((copies,)),
+            pltpu.SemaphoreType.DMA((sends,)), pltpu.SemaphoreType.DMA((arrivals,)),
         ],
         compiler_params=pltpu.CompilerParams(collective_id=0, has_side_effects=True, vmem_limit_bytes=67043328),
         name='gcn_step',

time: 127 us -> 124 us (0.976)
  Pallas kernels: 126 us -> 122 us
    pallas_call x1, Pallas kernels: 125 us -> 121 us  [device_step(): pl.pallas_call(step_kernel, out_shape=jax.ShapeDtypeStruct((SUM_ROWS, HID...]
where the time goes in v5:
time: 124 us; the launch traced here: 123 us
  Pallas kernels  122 us (98%)
    pallas_call x1, Pallas kernels, device_step(): pl.pallas_call(step_kernel, out_shape=jax.ShapeDtypeStruct((SUM_ROWS, HID...  121 us

profile of v5, /device:TPU:0, one launch (start us, length us, event | category | flops | bytes accessed | tf_op | source)
XLA Modules:
  0.0 123.4 jit_solution(18200036612326590969)
XLA Ops:
  0.6 121.0 %gcn_step.1.sums = f32[672,128]{1,0:T(8,128)} custom-call(bf16[2048,16384]{1,0:T(8,128)(2,1)} %adj.1, bf16[602,2048]{1,0:T(8,128)(2,1)} %bitcast.6, f32[602,128]{1,0:T(8,128)} %wh_in.1, f32[41,128]{1,0:T(8,128)} %bitcast.7, s32[1,2048]{1,0:T(1,128)} %bitcast.8, s32[1,2048]{1,0:T(1,128)} %bitcast.9, s32[8,8]{1,0:T(8,128)} %block_mask.1), custom_call_target="tpu_custom_call" | custom-call | tf_op jit(solution)/shard_map/gcn_step/pallas_call | solution.py:374
  121.7 0.0 copy-start
  121.7 1.0 copy-done
  122.6 0.7 cut.1
Async XLA Ops:
  121.7 1.0 copy-start

commit v6 on v5

--- a/solution.py
+++ b/solution.py
@@ -17,7 +17,7 @@
 C_PAD = 48
 HALF = ROWS // 2
 QUART = ROWS // 4
-SLOTS = 8
+SLOTS = 7
 CHUNKS = NODES // HALF
 SUM_ROWS = 672
 GWO_ROW = 608
@@ -56,15 +56,15 @@
             for i in range(2):
                 k, q = block_quart(g, i)
                 col = pl.multiple_of(partner(k) * ROWS + q * QUART, QUART)
-                self.pieces.append(pltpu.make_async_copy(adj.at[:, pl.ds(col, QUART)], abuf.at[slot, :, pl.ds(i * QUART, QUART)], asem.at[slot, i]))
+                self.pieces.append(pltpu.make_async_copy(adj.at[:, pl.ds(col, QUART)], abuf.at[slot, :, pl.ds(i * QUART, QUART)], asem.at[slot]))
+            self.whole = pltpu.make_async_copy(adj.at[:, pl.ds(0, HALF)], abuf.at[slot], asem.at[slot])
 
         def start(self):
             for piece in self.pieces:
                 piece.start()
 
         def wait(self):
-            for piece in self.pieces:
-                piece.wait()
+            self.whole.wait()
 
     fetch = Fetch
 
@@ -73,31 +73,21 @@
                                             device_id=(peers[k],), device_id_type=MESH)
 
     xcopy = pltpu.make_async_copy(feat, xbuf, xsem.at[0])
+    whcopy = pltpu.make_async_copy(wh_in, wh, xsem.at[1])
+    whcopy.start()
     xcopy.start()
-    small = [pltpu.make_async_copy(src, dst, xsem.at[1 + i]) for i, (src, dst) in
-             enumerate(((wh_in, wh), (wo_in, wo), (labels_in, labels), (mask_in, mask)))]
+    small = [pltpu.make_async_copy(src, dst, xsem.at[2 + i]) for i, (src, dst) in
+             enumerate(((wo_in, wo), (labels_in, labels), (mask_in, mask)))]
     for copy in small:
         copy.start()
-    fetch(jnp.int32(0)).start()
-    fetch(jnp.int32(1)).start()
     barrier = pltpu.get_barrier_semaphore()
     for k in range(1, DEVICES):
         pl.semaphore_signal(barrier, inc=1, device_id=(peers[k],), device_id_type=MESH)
-
-    for copy in small:
-        copy.wait()
-    wpad[...] = jnp.zeros_like(wpad)
-    wpad[:CLASSES, :] = wo[...]
-    wot_bf = wpad[:C_PAD, :].astype(BF16)
-    wo_bf = wpad[...].T[:, :C_PAD].astype(BF16)
+    whcopy.wait()
     wh_t = wh[...].T.astype(BF16)
-    weight = mask[...].astype(F32)
-    cnt[0] = jnp.broadcast_to(jnp.sum(weight, axis=1, keepdims=True), (8, 128))
     xcopy.wait()
-    for g in range(2, SLOTS - 2):
+    for g in range(SLOTS - 2):
         fetch(jnp.int32(g)).start()
-    yall[0] = jnp.dot(wh_t, xbuf[...], preferred_element_type=F32).astype(BF16)
-    pl.semaphore_wait(barrier, DEVICES - 1)
 
     def gather_copies(y, send, recv):
         def half(k, h):
@@ -124,11 +114,11 @@
         copies['sent'] = remote(y.at[pl.ds(0, 7)], y.at[pl.ds(0, 7)], 1, send, recv)
         return copies
 
-    def gather_start(copies):
-        for q in range(4):
+    def gather_start(copies, quarters=range(4)):
+        for q in quarters:
             copies['x', q].start()
             copies['y', q].start()
-            if q == 0:
+            if q == 3:
                 copies['own'].start()
 
     def gather_need(copies, c):
@@ -185,9 +175,21 @@
             lax.fori_loop(0, steps, step, 0)
 
     copies1 = gather_copies(yall, 0, 0)
-    gather_start(copies1)
+    for h in range(2):
+        at = pl.ds(h * HALF, HALF)
+        yall[0, :, at] = jnp.dot(wh_t, xbuf[:, at], preferred_element_type=F32).astype(BF16)
+        if h == 0:
+            pl.semaphore_wait(barrier, DEVICES - 1)
+        gather_start(copies1, (2 * h, 2 * h + 1))
     acc[...] = jnp.zeros_like(acc)
-    forward_pass(copies1, yall, 0, ((0, 2, 2), (4, 1, 1), (5, 2, 3), (11, 1, 5)))
+    for copy in small:
+        copy.wait()
+    wpad[...] = jnp.zeros_like(wpad)
+    wpad[:CLASSES, :] = wo[...]
+    wot_bf = wpad[:C_PAD, :].astype(BF16)
+    wo_bf = wpad[...].T[:, :C_PAD].astype(BF16)
+    cnt[0] = jnp.broadcast_to(jnp.sum(mask[...].astype(F32), axis=1, keepdims=True), (8, 128))
+    forward_pass(copies1, yall, 0, ((0, 2, 2), (4, 1, 12)))
 
     hid[...] = jnp.maximum(acc[...], 0.0).astype(BF16)
     y2all[0] = lax.dot_general(wot_bf, hid[...], NT, preferred_element_type=F32).astype(BF16)
@@ -293,10 +295,13 @@
         scatter_events(copies3, pa, ra, fa, c, {6: (('y', 0),), 7: (('x', 0),), 9: (('y', 1),), 11: (('x', 1),)})
         return carry
     lax.fori_loop(0, CHUNKS, pass3, 0)
-    d2t = jnp.concatenate([scatter_result(copies3, pa, ia, q) for q in range(4)], axis=1)
-    back = jnp.dot(wo_bf, d2t, preferred_element_type=F32)
-    lhs[...] = jnp.where(hidt[...].astype(F32) > 0.0, back, 0.0).astype(BF16)
-
+    copies2['sent'].wait_send()
+    d2t = y2all.at[0]
+    for q in range(4):
+        at = pl.ds(q * QUART, QUART)
+        d2t[:, at] = scatter_result(copies3, pa, ia, q)
+        back = jnp.dot(wo_bf, d2t[:, at], preferred_element_type=F32)
+        lhs[:, at] = jnp.where(hidt[:, at].astype(F32) > 0.0, back, 0.0).astype(BF16)
     copies3['sent'].wait_send()
 
     copies4 = scatter_copies(pb, rb, fb, ib, 4, 43)
@@ -317,13 +322,13 @@
     lax.fori_loop(0, CHUNKS, pass4, 0)
 
     gpart[F_IN // 8 * 8:GWO_ROW, :] = jnp.zeros((8, HID), F32)
-    gpart[GWO_ROW:LOSS_ROW, :] = jnp.dot(d2t, hid[...], preferred_element_type=F32)
+    gpart[GWO_ROW:LOSS_ROW, :] = jnp.dot(d2t[...], hid[...], preferred_element_type=F32)
     gpart[LOSS_ROW:SUM_ROWS, :] = jnp.broadcast_to(loss / label_count, (SUM_ROWS - LOSS_ROW, HID))
-    copies2['sent'].wait_send()
     counts.wait_send()
-    for q in range(4):
-        term = lax.dot_general(xbuf[:, q * QUART:(q + 1) * QUART], scatter_result(copies4, pb, ib, q), NT, preferred_element_type=F32)
-        if q == 0:
+    for h in range(2):
+        d1t = jnp.concatenate([scatter_result(copies4, pb, ib, 2 * h + q) for q in range(2)], axis=1)
+        term = lax.dot_general(xbuf[:, h * HALF:(h + 1) * HALF], d1t, NT, preferred_element_type=F32)
+        if h == 0:
             gpart[:F_IN, :] = term
         else:
             gpart[:F_IN, :] += term
@@ -353,10 +358,8 @@
                 first[1][n].start()
     final = remote(gpart.at[mine, :], sums_out.at[mine, :], 1, 14, 68)
     final.start()
-    keep = pltpu.make_async_copy(gpart.at[mine, :], sums_out.at[mine, :], xsem.at[0])
-    keep.start()
+    sums_out[mine, :] = gpart[mine, :]
     copies4['sent'].wait_send()
-    keep.wait()
     final.wait()
 
 
@@ -373,9 +376,9 @@
     sends, arrivals = 15, 69
     sums = pl.pallas_call(
         step_kernel,
-        out_shape=jax.ShapeDtypeStruct((SUM_ROWS, HID), F32),
+        out_shape=pltpu.VMEM((SUM_ROWS, HID), F32),
         in_specs=[hbm] * 6 + [pl.BlockSpec(memory_space=pltpu.SMEM)],
-        out_specs=hbm,
+        out_specs=vmem,
         scratch_shapes=[
             v((SLOTS, ROWS, HALF), BF16), v((F_IN, ROWS), BF16), v((F_IN, HID), F32), v((CLASSES, HID), F32), v((1, ROWS), jnp.int32), v((1, ROWS), jnp.int32), v((ROWS, HID), F32),
             v((DEVICES, HID, ROWS), BF16), v((DEVICES, C_PAD, ROWS), BF16), v((HID, ROWS), BF16), v((ROWS, HID), BF16),
@@ -384,10 +387,10 @@
             v((4, 2, C_PAD, HALF), F32), v((2, 2, C_PAD, QUART), F32), v((2, 4, C_PAD, QUART), F32),
             v((DEVICES, HID, ROWS), F32), v((4, 2, HID, HALF), F32), v((2, 2, HID, QUART), F32), v((2, 4, HID, QUART), F32),
             v((SUM_ROWS, HID), F32), v((SUM_ROWS // 2, HID), F32), v((2, 2, SUM_ROWS // 4, HID), F32),
-            pltpu.SemaphoreType.DMA((SLOTS, 2)), pltpu.SemaphoreType.DMA((5,)),
+            pltpu.SemaphoreType.DMA((SLOTS,)), pltpu.SemaphoreType.DMA((5,)),
             pltpu.SemaphoreType.DMA((sends,)), pltpu.SemaphoreType.DMA((arrivals,)),
         ],
-        compiler_params=pltpu.CompilerParams(collective_id=0, has_side_effects=True, vmem_limit_bytes=67043328),
+        compiler_params=pltpu.CompilerParams(collective_id=0, has_side_effects=True, vmem_limit_bytes=62 * 2**20),
         name='gcn_step',
     )(adj, feat.T, w_hidden, w_output.T, labels.reshape(1, ROWS), train_mask.reshape(1, ROWS), block_mask)
     loss, gwh, gwo = pl.pallas_call(

time: 124 us -> 122 us (0.984)
  no operation moved by 1% of the time
where the time goes in v6:
time: 122 us
  Pallas kernels  122 us (100%)
    pallas_call x1, Pallas kernels, device_step(): pl.pallas_call(step_kernel, out_shape=pltpu.VMEM((SUM_ROWS, HID), F32), i...  121 us

profile of v6, /device:TPU:0, one launch (start us, length us, event | category | flops | bytes accessed | tf_op | source)
XLA Modules:
  0.0 122.3 jit_solution(14136923822779541574)
XLA Ops:
  0.6 120.9 %gcn_step.1.sums = f32[672,128]{1,0:T(8,128)S(1)} custom-call(bf16[2048,16384]{1,0:T(8,128)(2,1)} %adj.1, bf16[602,2048]{1,0:T(8,128)(2,1)} %bitcast.6, f32[602,128]{1,0:T(8,128)} %wh_in.1, f32[41,128]{1,0:T(8,128)} %bitcast.7, s32[1,2048]{1,0:T(1,128)} %bitcast.8, s32[1,2048]{1,0:T(1,128)} %bitcast.9, s32[8,8]{1,0:T(8,128)} %block_mask.1), custom_call_target="tpu_custom_call" | custom-call | tf_op jit(solution)/shard_map/gcn_step/pallas_call | solution.py:377
  121.5 0.7 cut.1

commit v7 on v6

--- a/solution.py
+++ b/solution.py
@@ -25,6 +25,14 @@
 NT = (((1,), (1,)), ((), ()))
 
 
+def div(a, b):
+    return a // b if isinstance(a, int) else lax.div(a, b)
+
+
+def rem(a, b):
+    return a % b if isinstance(a, int) else lax.rem(a, b)
+
+
 def step_kernel(adj, feat, wh_in, wo_in, labels_in, mask_in, block_mask, sums_out,
                 abuf, xbuf, wh, wo, labels, mask, acc, yall, y2all, ymask, hid, hidt, wpad, lhs, cnt,
                 ra, fa, ia, pb, rb, fb, ib, gpart, gpair, gacross,
@@ -33,38 +41,34 @@
     bits = (lax.rem(me, 2), lax.rem(me // 2, 2), me // 4)
 
     def partner(k):
-        return lax.rem(bits[0] + k, 2) + 2 * lax.rem(bits[1] + k // 2, 2) + 4 * lax.rem(bits[2] + k // 4, 2)
+        return lax.rem(bits[0] + k, 2) + 2 * lax.rem(bits[1] + div(k, 2), 2) + 4 * lax.rem(bits[2] + div(k, 4), 2)
 
     peers = [partner(k) for k in range(DEVICES)]
 
     def block_quart(g, i):
-        back = lax.div(g, 2 * CHUNKS)
-        c = lax.rem(g, CHUNKS)
-        q, r = lax.div(c, 4), lax.rem(c, 4)
-        mid = lax.div(q * (3 - q), 2)
-        last = lax.div(q, 3)
-        pair, odd = lax.div(c, 2), lax.rem(c, 2)
+        back = div(g, 2 * CHUNKS)
+        c = rem(g, CHUNKS)
+        q, r = div(c, 4), rem(c, 4)
+        mid = div(q * (3 - q), 2)
+        last = div(q, 3)
+        pair, odd = div(c, 2), rem(c, 2)
         forth_k = mid * (2 + odd + 2 * i) + (1 - mid) * (last * (6 + odd) + (1 - last) * pair)
         forth_q = mid * (pair - 2) + (1 - mid) * (2 * (last * (pair - 6) + (1 - last) * odd) + i)
-        back_k, back_h = mid * (5 - r) + (1 - mid) * (7 - 6 * last - odd), mid * (q - 1) + (1 - mid) * lax.div(r, 2)
+        back_k, back_h = mid * (5 - r) + (1 - mid) * (7 - 6 * last - odd), mid * (q - 1) + (1 - mid) * div(r, 2)
         return back * back_k + (1 - back) * forth_k, back * (2 * back_h + i) + (1 - back) * forth_q
 
     class Fetch:
         def __init__(self, g):
-            slot = lax.rem(g, SLOTS)
-            self.pieces = []
-            for i in range(2):
-                k, q = block_quart(g, i)
+            self.g, self.slot = g, rem(g, SLOTS)
+
+        def start(self, pieces=(0, 1)):
+            for i in pieces:
+                k, q = block_quart(self.g, i)
                 col = pl.multiple_of(partner(k) * ROWS + q * QUART, QUART)
-                self.pieces.append(pltpu.make_async_copy(adj.at[:, pl.ds(col, QUART)], abuf.at[slot, :, pl.ds(i * QUART, QUART)], asem.at[slot]))
-            self.whole = pltpu.make_async_copy(adj.at[:, pl.ds(0, HALF)], abuf.at[slot], asem.at[slot])
-
-        def start(self):
-            for piece in self.pieces:
-                piece.start()
+                pltpu.make_async_copy(adj.at[:, pl.ds(col, QUART)], abuf.at[self.slot, :, pl.ds(i * QUART, QUART)], asem.at[self.slot]).start()
 
         def wait(self):
-            self.whole.wait()
+            pltpu.make_async_copy(adj.at[:, pl.ds(0, HALF)], abuf.at[self.slot], asem.at[self.slot]).wait()
 
     fetch = Fetch
 
@@ -72,22 +76,21 @@
         return pltpu.make_async_remote_copy(src_ref=src, dst_ref=dst, send_sem=ssem.at[send], recv_sem=rsem.at[recv],
                                             device_id=(peers[k],), device_id_type=MESH)
 
-    xcopy = pltpu.make_async_copy(feat, xbuf, xsem.at[0])
+    xcopies = [pltpu.make_async_copy(feat.at[:, pl.ds(q * QUART, QUART)], xbuf.at[:, pl.ds(q * QUART, QUART)], xsem.at[5 + q]) for q in range(4)]
     whcopy = pltpu.make_async_copy(wh_in, wh, xsem.at[1])
     whcopy.start()
-    xcopy.start()
+    for copy in xcopies:
+        copy.start()
     small = [pltpu.make_async_copy(src, dst, xsem.at[2 + i]) for i, (src, dst) in
              enumerate(((wo_in, wo), (labels_in, labels), (mask_in, mask)))]
     for copy in small:
         copy.start()
+    fetch(0).start()
     barrier = pltpu.get_barrier_semaphore()
     for k in range(1, DEVICES):
         pl.semaphore_signal(barrier, inc=1, device_id=(peers[k],), device_id_type=MESH)
     whcopy.wait()
     wh_t = wh[...].T.astype(BF16)
-    xcopy.wait()
-    for g in range(SLOTS - 2):
-        fetch(jnp.int32(g)).start()
 
     def gather_copies(y, send, recv):
         def half(k, h):
@@ -144,68 +147,81 @@
     def mask_value(k):
         return block_mask[me, partner(k)].astype(F32)
 
-    def forward_pass(copies, y, first, segments):
+    def multiply(y, chunks):
         width = y.shape[1]
-        for begin, per_step, steps in segments:
-            def step(i, carry, begin=begin, per_step=per_step, steps=steps):
-                for at in range(steps):
-                    needs = [begin + at * per_step + j for j in range(per_step)]
-                    if any(c == 2 or c >= 4 for c in needs):
-                        @pl.when(i == at)
-                        def _(needs=needs):
-                            for c in needs:
-                                gather_need(copies, c)
-                total = None
-                for j in range(per_step):
-                    c = begin + i * per_step + j
-                    for part in range(2):
-                        k, q = block_quart(c, part)
-                        cols = pl.ds(pl.multiple_of(q * QUART, QUART), QUART)
-                        ymask[:width, (2 * j + part) * QUART:(2 * j + part + 1) * QUART] = (y[k, :, cols].astype(F32) * mask_value(k)).astype(BF16)
-                for j in range(per_step):
-                    fetch(first + begin + i * per_step + j).wait()
-                for j in range(per_step):
-                    fetch(first + begin + i * per_step + j + SLOTS - 2).start()
-                for j in range(per_step):
-                    g = first + begin + i * per_step + j
-                    term = lax.dot_general(abuf[lax.rem(g, SLOTS)], ymask[:width, j * HALF:(j + 1) * HALF], NT, preferred_element_type=F32)
-                    total = term if total is None else total + term
-                acc[:, :width] += total
-                return carry
-            lax.fori_loop(0, steps, step, 0)
+        for j, (g, quarters) in enumerate(chunks):
+            for part, (k, q) in enumerate(quarters):
+                cols = pl.ds(pl.multiple_of(q * QUART, QUART), QUART)
+                ymask[:width, (2 * j + part) * QUART:(2 * j + part + 1) * QUART] = (y[k, :, cols].astype(F32) * mask_value(k)).astype(BF16)
+        for g, _ in chunks:
+            fetch(g).wait()
+        for g, _ in chunks:
+            fetch(g + SLOTS - 2).start()
+        total = None
+        for j, (g, _) in enumerate(chunks):
+            term = lax.dot_general(abuf[rem(g, SLOTS)], ymask[:width, j * HALF:(j + 1) * HALF], NT, preferred_element_type=F32)
+            total = term if total is None else total + term
+        acc[:, :width] += total
 
     copies1 = gather_copies(yall, 0, 0)
-    for h in range(2):
-        at = pl.ds(h * HALF, HALF)
+    for q in range(4):
+        at = pl.ds(q * QUART, QUART)
+        xcopies[q].wait()
         yall[0, :, at] = jnp.dot(wh_t, xbuf[:, at], preferred_element_type=F32).astype(BF16)
-        if h == 0:
+        if q == 0:
+            fetch(1).start()
             pl.semaphore_wait(barrier, DEVICES - 1)
-        gather_start(copies1, (2 * h, 2 * h + 1))
+        gather_start(copies1, (q,))
+    for g in range(2, SLOTS - 2):
+        fetch(g).start()
     acc[...] = jnp.zeros_like(acc)
     for copy in small:
         copy.wait()
     wpad[...] = jnp.zeros_like(wpad)
     wpad[:CLASSES, :] = wo[...]
-    wot_bf = wpad[:C_PAD, :].astype(BF16)
-    wo_bf = wpad[...].T[:, :C_PAD].astype(BF16)
     cnt[0] = jnp.broadcast_to(jnp.sum(mask[...].astype(F32), axis=1, keepdims=True), (8, 128))
-    forward_pass(copies1, yall, 0, ((0, 2, 2), (4, 1, 12)))
+    def own_chip(c, carry):
+        @pl.when(c == 2)
+        def _():
+            gather_need(copies1, 2)
+        multiply(yall, [(c, [(lax.div(c, 2), 2 * lax.rem(c, 2) + i) for i in range(2)])])
+        return carry
+    lax.fori_loop(0, 4, own_chip, 0)
+
+    def need_at(j, steps, first):
+        for at in range(steps):
+            @pl.when(j == at)
+            def _(at=at):
+                gather_need(copies1, first + at)
+
+    def neighbours(j, carry):
+        need_at(j, 8, 4)
+        multiply(yall, [(4 + j, [(2 + lax.rem(j, 2) + 2 * i, lax.div(j, 2)) for i in range(2)])])
+        return carry
+    lax.fori_loop(0, 8, neighbours, 0)
+
+    def across(j, carry):
+        need_at(j, 4, 12)
+        multiply(yall, [(12 + j, [(6 + lax.rem(j, 2), 2 * lax.div(j, 2) + i) for i in range(2)])])
+        return carry
+    lax.fori_loop(0, 4, across, 0)
 
     hid[...] = jnp.maximum(acc[...], 0.0).astype(BF16)
-    y2all[0] = lax.dot_general(wot_bf, hid[...], NT, preferred_element_type=F32).astype(BF16)
-
-    copies2 = gather_copies(y2all, 1, 13)
+    y2all[0] = lax.dot_general(wpad[:C_PAD, :].astype(BF16), hid[...], NT, preferred_element_type=F32).astype(BF16)
+
+    copies2 = gather_copies(y2all, 1, 16)
     gather_start(copies2)
-    count_copies = [remote(cnt.at[0], cnt.at[k], k, 2, 26) for k in range(1, DEVICES)]
-    counts = remote(cnt.at[pl.ds(1, 7)], cnt.at[pl.ds(1, 7)], 1, 2, 26)
+    count_copies = [remote(cnt.at[0], cnt.at[k], k, 2, 32) for k in range(1, DEVICES)]
+    counts = remote(cnt.at[pl.ds(1, 7)], cnt.at[pl.ds(1, 7)], 1, 2, 32)
     for copy in count_copies:
         copy.start()
     copies1['sent'].wait_send()
-    ident = (lax.broadcasted_iota(jnp.int32, (HID, HID), 0) == lax.broadcasted_iota(jnp.int32, (HID, HID), 1)).astype(BF16)
-    hidt[...] = lax.dot_general(ident, hid[...], NT, preferred_element_type=F32).astype(BF16)
     acc[...] = jnp.zeros_like(acc)
 
-    forward_pass(copies2, y2all, CHUNKS, ((0, 2, 2), (4, 1, 1), (5, 2, 5), (15, 1, 1)))
+    for chunks in ((0, 1), (2, 3), (4,), (5, 6), (7, 8), (9, 10), (11, 12), (13, 14), (15,)):
+        for c in chunks:
+            gather_need(copies2, c)
+        multiply(y2all, [(CHUNKS + c, [block_quart(c, i) for i in range(2)]) for c in chunks])
 
     for i in range(ROWS // 128):
         at = pl.ds(i * 128, 128)
@@ -282,7 +298,7 @@
         return (p[0, :, pl.ds(q * QUART, QUART)] + ix[0, q] + ix[1, q]).astype(BF16)
 
     pa = pb.at[:, pl.ds(0, C_PAD), :]
-    copies3 = scatter_copies(pa, ra, fa, ia, 3, 27)
+    copies3 = scatter_copies(pa, ra, fa, ia, 3, 0)
 
     def pass3(c, carry):
         g = c + 2 * CHUNKS
@@ -290,11 +306,14 @@
         cols = pl.ds(pl.multiple_of(q * QUART, HALF), HALF)
         fetch(g).wait()
         fetch(g + SLOTS - 2).start()
-        part = jnp.dot(lhs[...], abuf[lax.rem(g, SLOTS)], preferred_element_type=F32)
+        part = jnp.dot(lhs[...], abuf[rem(g, SLOTS)], preferred_element_type=F32)
         pa[k, :, cols] = part[:C_PAD] * mask_value(k)
         scatter_events(copies3, pa, ra, fa, c, {6: (('y', 0),), 7: (('x', 0),), 9: (('y', 1),), 11: (('x', 1),)})
         return carry
     lax.fori_loop(0, CHUNKS, pass3, 0)
+    ident = (lax.broadcasted_iota(jnp.int32, (HID, HID), 0) == lax.broadcasted_iota(jnp.int32, (HID, HID), 1)).astype(BF16)
+    hidt[...] = lax.dot_general(ident, hid[...], NT, preferred_element_type=F32).astype(BF16)
+    wo_bf = wpad[...].T[:, :C_PAD].astype(BF16)
     copies2['sent'].wait_send()
     d2t = y2all.at[0]
     for q in range(4):
@@ -304,7 +323,7 @@
         lhs[:, at] = jnp.where(hidt[:, at].astype(F32) > 0.0, back, 0.0).astype(BF16)
     copies3['sent'].wait_send()
 
-    copies4 = scatter_copies(pb, rb, fb, ib, 4, 43)
+    copies4 = scatter_copies(pb, rb, fb, ib, 4, 16)
 
     def pass4(c, carry):
         g = c + 3 * CHUNKS
@@ -315,7 +334,7 @@
         @pl.when(g + SLOTS - 2 < 4 * CHUNKS)
         def _():
             fetch(g + SLOTS - 2).start()
-        part = jnp.dot(lhs[...], abuf[lax.rem(g, SLOTS)], preferred_element_type=F32)
+        part = jnp.dot(lhs[...], abuf[rem(g, SLOTS)], preferred_element_type=F32)
         pb[k, :, cols] = part * mask_value(k)
         scatter_events(copies4, pb, rb, fb, c, {9: (('y', 0),), 10: (('x', 0),), 13: (('y', 1), ('x', 1))})
         return carry
@@ -336,7 +355,7 @@
     half_rows, quart_rows = SUM_ROWS // 2, SUM_ROWS // 4
     mine = pl.ds(pl.multiple_of(bits[0] * half_rows, 8), half_rows)
     other = pl.ds(pl.multiple_of((1 - bits[0]) * half_rows, 8), half_rows)
-    swap = remote(gpart.at[other, :], gpair, 1, 5, 59)
+    swap = remote(gpart.at[other, :], gpair, 1, 0, 0)
     swap.start()
     swap.wait()
     gpart[mine, :] = gpart[mine, :] + gpair[...]
@@ -348,7 +367,7 @@
         rows.append(at)
         for step in range(2):
             way = (2, 4)[(q + step) % 2]
-            first[step][n] = remote(gpart.at[at, :], gacross.at[step, q, pl.ds(begin, size), :], way, 6 + 4 * step + n, 60 + 4 * step + n)
+            first[step][n] = remote(gpart.at[at, :], gacross.at[step, q, pl.ds(begin, size), :], way, 5 + 4 * step + n, 1 + 4 * step + n)
         first[0][n].start()
     for step in range(2):
         for n, (q, begin, size) in enumerate(pieces):
@@ -356,7 +375,7 @@
             gpart[rows[n], :] = gpart[rows[n], :] + gacross[step, q, begin:begin + size, :]
             if step == 0:
                 first[1][n].start()
-    final = remote(gpart.at[mine, :], sums_out.at[mine, :], 1, 14, 68)
+    final = remote(gpart.at[mine, :], sums_out.at[mine, :], 1, 1, 9)
     final.start()
     sums_out[mine, :] = gpart[mine, :]
     copies4['sent'].wait_send()
@@ -373,7 +392,7 @@
     vmem = pl.BlockSpec(memory_space=pltpu.VMEM)
     hbm = pl.BlockSpec(memory_space=pl.ANY)
     v = pltpu.VMEM
-    sends, arrivals = 15, 69
+    sends, arrivals = 13, 33
     sums = pl.pallas_call(
         step_kernel,
         out_shape=pltpu.VMEM((SUM_ROWS, HID), F32),
@@ -387,7 +406,7 @@
             v((4, 2, C_PAD, HALF), F32), v((2, 2, C_PAD, QUART), F32), v((2, 4, C_PAD, QUART), F32),
             v((DEVICES, HID, ROWS), F32), v((4, 2, HID, HALF), F32), v((2, 2, HID, QUART), F32), v((2, 4, HID, QUART), F32),
             v((SUM_ROWS, HID), F32), v((SUM_ROWS // 2, HID), F32), v((2, 2, SUM_ROWS // 4, HID), F32),
-            pltpu.SemaphoreType.DMA((SLOTS,)), pltpu.SemaphoreType.DMA((5,)),
+            pltpu.SemaphoreType.DMA((SLOTS,)), pltpu.SemaphoreType.DMA((9,)),
             pltpu.SemaphoreType.DMA((sends,)), pltpu.SemaphoreType.DMA((arrivals,)),
         ],
         compiler_params=pltpu.CompilerParams(collective_id=0, has_side_effects=True, vmem_limit_bytes=62 * 2**20),

time: 122 us -> 118 us (0.967)
  Pallas kernels: 122 us -> 117 us
    pallas_call x1, Pallas kernels: 121 us -> 117 us  [device_step(): pl.pallas_call(step_kernel, out_shape=pltpu.VMEM((SUM_ROWS, HID), F32), i...]
where the time goes in v7:
time: 118 us
  Pallas kernels  117 us (99%)
    pallas_call x1, Pallas kernels, device_step(): pl.pallas_call(step_kernel, out_shape=pltpu.VMEM((SUM_ROWS, HID), F32), i...  117 us

profile of v7, /device:TPU:0, one launch (start us, length us, event | category | flops | bytes accessed | tf_op | source)
XLA Modules:
  0.0 118.1 jit_solution(10226326310660464628)
XLA Ops:
  0.6 116.8 %gcn_step.1.sums = f32[672,128]{1,0:T(8,128)S(1)} custom-call(bf16[2048,16384]{1,0:T(8,128)(2,1)} %adj.1, bf16[602,2048]{1,0:T(8,128)(2,1)} %bitcast.6, f32[602,128]{1,0:T(8,128)} %wh_in.1, f32[41,128]{1,0:T(8,128)} %bitcast.7, s32[1,2048]{1,0:T(1,128)} %bitcast.8, s32[1,2048]{1,0:T(1,128)} %bitcast.9, s32[8,8]{1,0:T(8,128)} %block_mask.1), custom_call_target="tpu_custom_call" | custom-call | tf_op jit(solution)/shard_map/gcn_step/pallas_call | solution.py:396
  117.4 0.7 cut.1

commit v8 on v7

--- a/solution.py
+++ b/solution.py
@@ -23,6 +23,7 @@
 GWO_ROW = 608
 LOSS_ROW = GWO_ROW + C_PAD
 NT = (((1,), (1,)), ((), ()))
+BACK_ORDER = ((7, 0), (6, 0), (7, 1), (3, 0), (6, 1), (5, 0), (2, 0), (4, 0), (3, 1), (5, 1), (2, 1), (4, 1), (1, 0), (1, 1), (0, 0), (0, 1))
 
 
 def div(a, b):
@@ -48,14 +49,18 @@
     def block_quart(g, i):
         back = div(g, 2 * CHUNKS)
         c = rem(g, CHUNKS)
-        q, r = div(c, 4), rem(c, 4)
+        q = div(c, 4)
         mid = div(q * (3 - q), 2)
         last = div(q, 3)
         pair, odd = div(c, 2), rem(c, 2)
         forth_k = mid * (2 + odd + 2 * i) + (1 - mid) * (last * (6 + odd) + (1 - last) * pair)
         forth_q = mid * (pair - 2) + (1 - mid) * (2 * (last * (pair - 6) + (1 - last) * odd) + i)
-        back_k, back_h = mid * (5 - r) + (1 - mid) * (7 - 6 * last - odd), mid * (q - 1) + (1 - mid) * div(r, 2)
-        return back * back_k + (1 - back) * forth_k, back * (2 * back_h + i) + (1 - back) * forth_q
+        if isinstance(g, int):
+            return (BACK_ORDER[c][0], 2 * BACK_ORDER[c][1] + i) if back else (forth_k, forth_q)
+        code = jnp.int32(0)
+        for at, (k, h) in enumerate(BACK_ORDER):
+            code = jnp.where(c == at, 2 * k + h, code)
+        return back * div(code, 2) + (1 - back) * forth_k, back * (2 * rem(code, 2) + i) + (1 - back) * forth_q
 
     class Fetch:
         def __init__(self, g):
@@ -270,8 +275,7 @@
 
     def scatter_events(copies, p, r, f, c, pass_on):
         sends = {6: ('xy', 'yx'), 4: ('y raw',), 2: ('x raw',), 0: ()}
-        order = [(7, 0), (6, 0), (7, 1), (6, 1)] + [(k, h) for h in range(2) for k in (5, 4, 3, 2)] + [(1, 0), (0, 0), (1, 1), (0, 1)]
-        for at, (k, h) in enumerate(order):
+        for at, (k, h) in enumerate(BACK_ORDER):
             @pl.when(c == at)
             def _(at=at, k=k, h=h):
                 if k % 2 == 1:
@@ -308,7 +312,7 @@
         fetch(g + SLOTS - 2).start()
         part = jnp.dot(lhs[...], abuf[rem(g, SLOTS)], preferred_element_type=F32)
         pa[k, :, cols] = part[:C_PAD] * mask_value(k)
-        scatter_events(copies3, pa, ra, fa, c, {6: (('y', 0),), 7: (('x', 0),), 9: (('y', 1),), 11: (('x', 1),)})
+        scatter_events(copies3, pa, ra, fa, c, {7: (('x', 0), ('y', 0)), 10: (('x', 1),), 11: (('y', 1),)})
         return carry
     lax.fori_loop(0, CHUNKS, pass3, 0)
     ident = (lax.broadcasted_iota(jnp.int32, (HID, HID), 0) == lax.broadcasted_iota(jnp.int32, (HID, HID), 1)).astype(BF16)
@@ -336,7 +340,7 @@
             fetch(g + SLOTS - 2).start()
         part = jnp.dot(lhs[...], abuf[rem(g, SLOTS)], preferred_element_type=F32)
         pb[k, :, cols] = part * mask_value(k)
-        scatter_events(copies4, pb, rb, fb, c, {9: (('y', 0),), 10: (('x', 0),), 13: (('y', 1), ('x', 1))})
+        scatter_events(copies4, pb, rb, fb, c, {9: (('y', 0), ('x', 0)), 14: (('y', 1), ('x', 1))})
         return carry
     lax.fori_loop(0, CHUNKS, pass4, 0)
 

time: 118 us -> 118 us (level)
  no operation moved by 1% of the time
where the time goes in v8:
time: 118 us
  Pallas kernels  117 us (99%)
    pallas_call x1, Pallas kernels, device_step(): pl.pallas_call(step_kernel, out_shape=pltpu.VMEM((SUM_ROWS, HID), F32), i...  117 us

profile of v8, /device:TPU:0, one launch (start us, length us, event | category | flops | bytes accessed | tf_op | source)
XLA Modules:
  0.0 118.0 jit_solution(17966162064372016774)
XLA Ops:
  0.6 116.6 %gcn_step.1.sums = f32[672,128]{1,0:T(8,128)S(1)} custom-call(bf16[2048,16384]{1,0:T(8,128)(2,1)} %adj.1, bf16[602,2048]{1,0:T(8,128)(2,1)} %bitcast.6, f32[602,128]{1,0:T(8,128)} %wh_in.1, f32[41,128]{1,0:T(8,128)} %bitcast.7, s32[1,2048]{1,0:T(1,128)} %bitcast.8, s32[1,2048]{1,0:T(1,128)} %bitcast.9, s32[8,8]{1,0:T(8,128)} %block_mask.1), custom_call_target="tpu_custom_call" | custom-call | tf_op jit(solution)/shard_map/gcn_step/pallas_call | solution.py:400
  117.3 0.7 cut.1

commit v9 on v8

--- a/solution.py
+++ b/solution.py
@@ -364,14 +364,14 @@
     swap.wait()
     gpart[mine, :] = gpart[mine, :] + gpair[...]
     first = [{}, {}]
-    pieces = [(q, begin, size) for begin, size in ((0, 88), (88, quart_rows - 88)) for q in range(2)]
+    pieces = [(q, begin, size) for begin, size in ((0, 56), (56, 56), (112, 56)) for q in range(2)]
     rows = []
     for n, (q, begin, size) in enumerate(pieces):
         at = pl.ds(pl.multiple_of(bits[0] * half_rows + q * quart_rows + begin, 8), size)
         rows.append(at)
         for step in range(2):
             way = (2, 4)[(q + step) % 2]
-            first[step][n] = remote(gpart.at[at, :], gacross.at[step, q, pl.ds(begin, size), :], way, 5 + 4 * step + n, 1 + 4 * step + n)
+            first[step][n] = remote(gpart.at[at, :], gacross.at[step, q, pl.ds(begin, size), :], way, 5 + 6 * step + n, 1 + 6 * step + n)
         first[0][n].start()
     for step in range(2):
         for n, (q, begin, size) in enumerate(pieces):
@@ -379,7 +379,7 @@
             gpart[rows[n], :] = gpart[rows[n], :] + gacross[step, q, begin:begin + size, :]
             if step == 0:
                 first[1][n].start()
-    final = remote(gpart.at[mine, :], sums_out.at[mine, :], 1, 1, 9)
+    final = remote(gpart.at[mine, :], sums_out.at[mine, :], 1, 1, 13)
     final.start()
     sums_out[mine, :] = gpart[mine, :]
     copies4['sent'].wait_send()
@@ -396,7 +396,7 @@
     vmem = pl.BlockSpec(memory_space=pltpu.VMEM)
     hbm = pl.BlockSpec(memory_space=pl.ANY)
     v = pltpu.VMEM
-    sends, arrivals = 13, 33
+    sends, arrivals = 17, 33
     sums = pl.pallas_call(
         step_kernel,
         out_shape=pltpu.VMEM((SUM_ROWS, HID), F32),

time: 118 us -> 118 us (level)
  no operation moved by 1% of the time
where the time goes in v9:
time: 118 us
  Pallas kernels  118 us (100%)
    pallas_call x1, Pallas kernels, device_step(): pl.pallas_call(step_kernel, out_shape=pltpu.VMEM((SUM_ROWS, HID), F32), i...  117 us

profile of v9, /device:TPU:0, one launch (start us, length us, event | category | flops | bytes accessed | tf_op | source)
XLA Modules:
  0.0 118.2 jit_solution(3139547951542312406)
XLA Ops:
  0.6 116.8 %gcn_step.1.sums = f32[672,128]{1,0:T(8,128)S(1)} custom-call(bf16[2048,16384]{1,0:T(8,128)(2,1)} %adj.1, bf16[602,2048]{1,0:T(8,128)(2,1)} %bitcast.6, f32[602,128]{1,0:T(8,128)} %wh_in.1, f32[41,128]{1,0:T(8,128)} %bitcast.7, s32[1,2048]{1,0:T(1,128)} %bitcast.8, s32[1,2048]{1,0:T(1,128)} %bitcast.9, s32[8,8]{1,0:T(8,128)} %block_mask.1), custom_call_target="tpu_custom_call" | custom-call | tf_op jit(solution)/shard_map/gcn_step/pallas_call | solution.py:400
  117.4 0.7 cut.1
